TPU v7x, 32 devices: a whole 2x2x4 slice. The times are simulated.
32 devices in a mesh: depth: 8 (over y, x, core), screen: 4 (over z).
Axes of the slice: x: 2, y: 2, z: 4, core: 2. Of those that a mesh axis runs over, the one named last changes fastest.
Arguments:
- block_tile: int32 [8, 8192], P('depth', 'screen'), may hold values from 0 to 127
- block_count: int32 [8, 4], P('depth', 'screen'), may hold values from 256 to 2048, as said below
- slab_rank: int32 [8], replicated, may hold values from 0 to 7, each once
- corner: int32 [2, 8, 8192, 128], P(None, 'depth', 'screen'), may hold values from 0 to 16
- offset: float32 [2, 8, 8192, 128], P(None, 'depth', 'screen'), may hold values from 0.25 to 0.75
- radius: float32 [8, 8192, 128], P('depth', 'screen'), may hold values from 3 to 8
- emission: float32 [3, 8, 8192, 128], P(None, 'depth', 'screen'), may hold values from 0.002 to 0.02
- extinction: float32 [8, 8192, 128], P('depth', 'screen'), may hold values from 0.001 to 0.01
Outputs:
- image_tiles: float32 [128, 32, 128], P(('depth', 'screen'))
Inputs may be any that keep to these rules, and one draw needn't show every extreme that they name: The live slots of a device are its first block_count slots; one device of every draw has all 2048 slots live. `block_tile`: a block holds particles of one tile. `corner`: a footprint box lies inside its tile. `slab_rank`: each slab once.
All inputs are finite; a program needn't handle non-finite values.
Results may differ from a plain program's by a relative error of at most 0.0003.
Values sent between devices are 32-bit elements; how exact they have to be, the bound alone decides.
No kernel may reach another device: no remote copies, remote signals or barrier semaphores. Data moves between devices by JAX's collectives and lax.ppermute only.
A program may use at most 128 MiB of HBM per device.

v0:
```python
import jax
import jax.numpy as jnp
from jax import lax
from jax.sharding import PartitionSpec as P

TS = 32
FOOT = 16
TILE_DEV = 4


def axis_weights(corner, offset, radius, tile_side, foot):
    pixel_index = jnp.arange(tile_side, dtype=jnp.int32)
    pixel_centre = pixel_index.astype(jnp.float32) + 0.5
    centres = corner.astype(jnp.float32) + foot * offset
    scaled = (pixel_centre - centres[..., None]) / radius[..., None]
    bump_shape = jnp.maximum(1.0 - scaled * scaled, 0.0)
    inside = (pixel_index >= corner[..., None]) & (pixel_index < corner[..., None] + foot)
    return jnp.where(inside, bump_shape * bump_shape, 0.0)


def deposit(corner, offset, radius, emission, extinction, block_live, tile_side, foot):
    across = axis_weights(corner[0], offset[0], radius, tile_side, foot)
    down_weights = axis_weights(corner[1], offset[1], radius, tile_side, foot)
    fields = jnp.concatenate([emission, extinction[None]], 0) * block_live[None, :, None]
    spread = fields[..., None] * across[None]
    deposit_out = jnp.einsum(
        "gpy,cgpx->gycx", down_weights, spread, precision=lax.Precision.HIGHEST
    )
    return deposit_out.reshape(deposit_out.shape[0], tile_side, 4 * tile_side)


def composite(stacked, slab_rank):
    slab_num, tile_num, tile_side, row_width = stacked.shape
    pieces = stacked.reshape(slab_num, tile_num, tile_side, 4, row_width // 4)
    glow_part = pieces[:, :, :, :3, :]
    optical = pieces[:, :, :, 3:, :]
    before = (slab_rank[None, :] < slab_rank[:, None]).astype(jnp.float32)
    prior_depth = jnp.einsum("jk,ktyax->jtyax", before, optical, precision=lax.Precision.HIGHEST)
    lighting = jnp.sum(jnp.exp(-prior_depth) * glow_part * jnp.exp(-0.5 * optical), axis=0)
    coverage = 1.0 - jnp.exp(-jnp.sum(optical, axis=0))
    return jnp.concatenate([lighting, coverage], axis=2).reshape(tile_num, tile_side, row_width)


def shards(block_tile, block_count, slab_rank, corner, offset, radius, emission, extinction):
    slots = block_tile.shape[1]
    group_size = min(256, slots)
    depth_size = lax.axis_size("depth")
    screen_size = lax.axis_size("screen")
    tiles_all = TILE_DEV * depth_size * screen_size
    live_count = block_count[0, 0]
    rounds = (live_count + group_size - 1) // group_size

    def one_round(round_index, tile_sums):
        first_row = round_index * group_size
        ids_now = lax.dynamic_slice_in_dim(block_tile[0], first_row, group_size, 0)
        corner_now = lax.dynamic_slice_in_dim(corner[:, 0], first_row, group_size, 1)
        offset_now = lax.dynamic_slice_in_dim(offset[:, 0], first_row, group_size, 1)
        radius_now = lax.dynamic_slice_in_dim(radius[0], first_row, group_size, 0)
        glow_now = lax.dynamic_slice_in_dim(emission[:, 0], first_row, group_size, 1)
        rate_now = lax.dynamic_slice_in_dim(extinction[0], first_row, group_size, 0)
        live_now = (first_row + jnp.arange(group_size, dtype=jnp.int32) < live_count).astype(
            jnp.float32
        )
        deposit_out = deposit(
            corner_now, offset_now, radius_now, glow_now, rate_now, live_now, TS, FOOT
        )
        return tile_sums.at[ids_now].add(deposit_out)

    partial_value = lax.fori_loop(
        0, rounds, one_round, jnp.zeros((tiles_all, TS, 4 * TS), jnp.float32)
    )
    shaped = partial_value.reshape(depth_size, screen_size * TILE_DEV, TS, 4 * TS)
    owned = lax.psum_scatter(shaped, "screen", scatter_dimension=1, tiled=True)
    return composite(
        lax.all_to_all(owned, "depth", split_axis=0, concat_axis=0, tiled=True), slab_rank
    )


def solution(mesh):
    placed = (
        P("depth", "screen"),
        P("depth", "screen"),
        P(),
        P(None, "depth", "screen", None),
        P(None, "depth", "screen", None),
        P("depth", "screen", None),
        P(None, "depth", "screen", None),
        P("depth", "screen", None),
    )
    return jax.shard_map(
        shards,
        mesh=mesh,
        in_specs=placed,
        out_specs=P(("depth", "screen"), None, None),
        check_vma=False,
    )
```

profile of v0, /device:TPU:0, one launch (start us, length us, event | category | flops | bytes accessed | tf_op | source)
XLA Modules:
  0.0 1155.8 jit_solution(5057850050785200805)
XLA Ops:
  7.5 517.1 %while.10 = (s32[]{:T(128)}, f32[128,32,128]{2,1,0:T(8,128)S(1)}, s32[]{:T(128)}, s32[1,2048]{1,0:T(1,128)}, s32[2,1,2048,128]{3,2,1,0:T(8,128)}, /*index=5*/f32...) while((s32[]{:T(128)}, f32[128,32,128]{2,1,0:T(8,128)S(1)}, ...), condition=%wide.region_2.3_spmd, body=%wide.region_0.2_spmd.sunk | while | flops 1637353088 | bytes 48240240 | solution.py:69
  10.5 1.8 multiply_select_fusion.2
  15.5 79.2 %fusion.46 = f32[256,32,4,32]{3,1,2,0:T(8,128)} fusion(f32[256,128,32]{1,2,0:T(8,128)S(1)} %multiply_select_fusion.2, f32[4,256,128]{2,0,1:T(4,128)S(1)} %maximum_multiply_fusion.2, f32[256,128]{1,0:T(8,128)S(1)} %dynamic-slice_bitcast_fusion.6, f32[256,128]{1,0:T(8,128)S(1)} %get-tuple-element.201, f32[32]{0:T(128)S(1)} %convert_add_fusion.2, ...), kind=kOutput, calls=%fused_computation.1.clone.1 | convolution fusion | flops 1625292800 | bytes 9437312 | tf_op jit(solution)/shard_map/while/body/gpy,cgpx->gycx/dot_general | solution.py:26
  94.8 13.3 %copy.49 = f32[256,32,4,32]{0,3,2,1:T(8,128)} copy(f32[256,32,4,32]{3,1,2,0:T(8,128)} %fusion.46) | data formatting | bytes 8388608 | tf_op jit(solution)/shard_map/while/body/gpy,cgpx->gycx/dot_general | solution.py:26
  108.1 5.5 copy.50
  114.3 22.4 %scatter_fusion = f32[128,32,128]{2,1,0:T(8,128)S(1)} fusion(f32[128,32,128]{2,1,0:T(8,128)S(1)} %get-tuple-element.219, s32[256]{0:T(256)S(1)} %bitcast.73, f32[256,32,128]{2,1,0:T(8,128)} %copy.50), kind=kCustom, calls=%fused_computation.clone.1 | custom fusion | flops 1048576 | bytes 12583936 | tf_op jit(solution)/shard_map/while/body/scatter-add | solution.py:67
  139.7 1.8 multiply_select_fusion.2
  144.8 79.3 %fusion.46 = f32[256,32,4,32]{3,1,2,0:T(8,128)} fusion(f32[256,128,32]{1,2,0:T(8,128)S(1)} %multiply_select_fusion.2, f32[4,256,128]{2,0,1:T(4,128)S(1)} %maximum_multiply_fusion.2, f32[256,128]{1,0:T(8,128)S(1)} %dynamic-slice_bitcast_fusion.6, f32[256,128]{1,0:T(8,128)S(1)} %get-tuple-element.201, f32[32]{0:T(128)S(1)} %convert_add_fusion.2, ...), kind=kOutput, calls=%fused_computation.1.clone.1 | convolution fusion | flops 1625292800 | bytes 9437312 | tf_op jit(solution)/shard_map/while/body/gpy,cgpx->gycx/dot_general | solution.py:26
  224.0 13.3 %copy.49 = f32[256,32,4,32]{0,3,2,1:T(8,128)} copy(f32[256,32,4,32]{3,1,2,0:T(8,128)} %fusion.46) | data formatting | bytes 8388608 | tf_op jit(solution)/shard_map/while/body/gpy,cgpx->gycx/dot_general | solution.py:26
  237.3 5.5 copy.50
  243.5 22.4 %scatter_fusion = f32[128,32,128]{2,1,0:T(8,128)S(1)} fusion(f32[128,32,128]{2,1,0:T(8,128)S(1)} %get-tuple-element.219, s32[256]{0:T(256)S(1)} %bitcast.73, f32[256,32,128]{2,1,0:T(8,128)} %copy.50), kind=kCustom, calls=%fused_computation.clone.1 | custom fusion | flops 1048576 | bytes 12583936 | tf_op jit(solution)/shard_map/while/body/scatter-add | solution.py:67
  268.9 1.8 multiply_select_fusion.2
  274.0 79.2 %fusion.46 = f32[256,32,4,32]{3,1,2,0:T(8,128)} fusion(f32[256,128,32]{1,2,0:T(8,128)S(1)} %multiply_select_fusion.2, f32[4,256,128]{2,0,1:T(4,128)S(1)} %maximum_multiply_fusion.2, f32[256,128]{1,0:T(8,128)S(1)} %dynamic-slice_bitcast_fusion.6, f32[256,128]{1,0:T(8,128)S(1)} %get-tuple-element.201, f32[32]{0:T(128)S(1)} %convert_add_fusion.2, ...), kind=kOutput, calls=%fused_computation.1.clone.1 | convolution fusion | flops 1625292800 | bytes 9437312 | tf_op jit(solution)/shard_map/while/body/gpy,cgpx->gycx/dot_general | solution.py:26
  353.3 13.3 %copy.49 = f32[256,32,4,32]{0,3,2,1:T(8,128)} copy(f32[256,32,4,32]{3,1,2,0:T(8,128)} %fusion.46) | data formatting | bytes 8388608 | tf_op jit(solution)/shard_map/while/body/gpy,cgpx->gycx/dot_general | solution.py:26
  366.6 5.5 copy.50
  372.7 22.4 %scatter_fusion = f32[128,32,128]{2,1,0:T(8,128)S(1)} fusion(f32[128,32,128]{2,1,0:T(8,128)S(1)} %get-tuple-element.219, s32[256]{0:T(256)S(1)} %bitcast.73, f32[256,32,128]{2,1,0:T(8,128)} %copy.50), kind=kCustom, calls=%fused_computation.clone.1 | custom fusion | flops 1048576 | bytes 12583936 | tf_op jit(solution)/shard_map/while/body/scatter-add | solution.py:67
  398.2 1.8 multiply_select_fusion.2
  403.2 79.2 %fusion.46 = f32[256,32,4,32]{3,1,2,0:T(8,128)} fusion(f32[256,128,32]{1,2,0:T(8,128)S(1)} %multiply_select_fusion.2, f32[4,256,128]{2,0,1:T(4,128)S(1)} %maximum_multiply_fusion.2, f32[256,128]{1,0:T(8,128)S(1)} %dynamic-slice_bitcast_fusion.6, f32[256,128]{1,0:T(8,128)S(1)} %get-tuple-element.201, f32[32]{0:T(128)S(1)} %convert_add_fusion.2, ...), kind=kOutput, calls=%fused_computation.1.clone.1 | convolution fusion | flops 1625292800 | bytes 9437312 | tf_op jit(solution)/shard_map/while/body/gpy,cgpx->gycx/dot_general | solution.py:26
  482.5 13.3 %copy.49 = f32[256,32,4,32]{0,3,2,1:T(8,128)} copy(f32[256,32,4,32]{3,1,2,0:T(8,128)} %fusion.46) | data formatting | bytes 8388608 | tf_op jit(solution)/shard_map/while/body/gpy,cgpx->gycx/dot_general | solution.py:26
  495.8 5.5 copy.50
  502.0 22.4 %scatter_fusion = f32[128,32,128]{2,1,0:T(8,128)S(1)} fusion(f32[128,32,128]{2,1,0:T(8,128)S(1)} %get-tuple-element.219, s32[256]{0:T(256)S(1)} %bitcast.73, f32[256,32,128]{2,1,0:T(8,128)} %copy.50), kind=kCustom, calls=%fused_computation.clone.1 | custom fusion | flops 1048576 | bytes 12583936 | tf_op jit(solution)/shard_map/while/body/scatter-add | solution.py:67
  524.6 1.3 copy-done
  527.2 602.2 %all-reduce.3.cloned.1.call-done = f32[8,16,32,128]{3,2,1,0:T(8,128)} async-done(((f32[8,16,32,128]{3,2,1,0:T(8,128)}), f32[8,16,32,128]{3,2,1,0:T(8,128)}) %all-reduce.3.cloned.1.call-update) | async-done | bytes 2097168
  1130.5 13.2 %all_to_all.5 = f32[8,4,32,128]{3,2,1,0:T(8,128)S(1)} all-to-all(f32[8,4,32,128]{3,2,1,0:T(8,128)S(1)} %constant_dynamic-slice_fusion.3), channel_id=1, replica_groups=mesh['depth'=8,'screen'=4] {'depth'}, dimensions={0} | all-to-all | bytes 1048576 | tf_op jit(solution)/shard_map/all_to_all | solution.py:75
  (60 shorter events, 34.5 us)
Async XLA Ops:
  6.5 1122.9 %all-reduce.3.cloned.1.call-start = ((), (), s32[]{:S(2)}) async-start(), calls=%async_computation.1 | async-start | bytes 4194304
  7.5 518.5 %copy-start.2 = (u32[32]{0:T(128)S(1)}, u32[32]{0:T(128)}, u32[]{:S(2)}) copy-start(u32[32]{0:T(128)} %constant.64) | copy-start | bytes 388
  524.6 1.3 copy-start
  524.6 621.3 %copy-start.1 = (s32[8]{0:T(128)S(1)}, s32[8]{0:T(128)}, u32[]{:S(2)}) copy-start(s32[8]{0:T(128)} %param.12) | copy-start | bytes 100
Sparse Core Ops, SparseCore 0:
  526.0 603.3 all-reduce.2
where the time goes:
time: 1160 us
  waiting for transfers between devices  602 us (52%)
  matrix products  318 us (27%)
  other arithmetic  114 us (10%)
  local copies, waits for them, and re-layouts  92.9 us (8%)
  between operations  14.8 us (1%)
  blocking collectives  13.2 us (1%)
    unnamed x2, waiting for transfers between devices  602 us
    dot_general x4, matrix products, deposit(): jnp.einsum('gpy,cgpx->gycx', down_weights, spread, precision=lax.Precisio...  317 us
    scatter-add x4, other arithmetic, one_round(): return tile_sums.at[ids_now].add(deposit_out)  89.7 us
    dot_general x4, local copies, waits for them, and re-layouts, deposit(): jnp.einsum('gpy,cgpx->gycx', down_weights, spread, precision=lax.Precisio...  53.2 us
  transfers between devices with their start and end apart: 1, of which 1 were waited for; matrix products, arithmetic and copies ran while one was open for 0% of the time, Pallas kernels for 0%

commit v1 on v0

v1 whole, which is shorter than its diff:
```python
import functools

import jax
import jax.numpy as jnp
from jax import lax
from jax.experimental import pallas as pl
from jax.experimental.pallas import tpu as pltpu
from jax.sharding import PartitionSpec as P

TS = 32
FOOT = 16
TILE_DEV = 4
N_CHUNK = 16
UNROLL = 16


def deposit_kernel(tiles_all, slots, pb, count_ref, tile_ref, corner_hbm, offset_hbm, radius_hbm,
                   emission_hbm, extinction_hbm, out_ref,
                   corner_v, offset_v, radius_v, emission_v, extinction_v, prep, acc, sems):
    rows = slots // N_CHUNK
    live_count = count_ref[0, 0]

    def copies(chunk):
        sl = pl.ds(pl.multiple_of(chunk * rows, rows), rows)
        return [
            pltpu.make_async_copy(corner_hbm.at[:, 0, sl], corner_v.at[:, sl], sems.at[chunk, 0]),
            pltpu.make_async_copy(offset_hbm.at[:, 0, sl], offset_v.at[:, sl], sems.at[chunk, 1]),
            pltpu.make_async_copy(radius_hbm.at[0, sl], radius_v.at[sl], sems.at[chunk, 2]),
            pltpu.make_async_copy(emission_hbm.at[:, 0, sl], emission_v.at[:, sl], sems.at[chunk, 3]),
            pltpu.make_async_copy(extinction_hbm.at[0, sl], extinction_v.at[sl], sems.at[chunk, 4]),
        ]

    def start_chunk(chunk, carry):
        for copy in copies(chunk):
            copy.start()
        return carry

    lax.fori_loop(0, N_CHUNK, start_chunk, 0)

    def clear(t, carry):
        acc[t] = jnp.zeros((4 * TS, 2 * TS), jnp.float32)
        return carry

    lax.fori_loop(0, tiles_all, clear, 0)

    pixel = lax.broadcasted_iota(jnp.int32, (TS, pb), 0).astype(jnp.float32)
    half = FOOT
    low_pixel = pixel[:half]
    high_pixel = pixel[half:] - float(FOOT)

    def bump(edge, centre, h2):
        s = pixel - centre
        p = h2 - s * s
        inside = jnp.concatenate([low_pixel >= edge, high_pixel < edge], axis=0)
        p = jnp.maximum(jnp.where(inside, p, 0.0), 0.0)
        return p * p

    def split(value):
        high = value.astype(jnp.bfloat16)
        low = (value - high.astype(jnp.float32)).astype(jnp.bfloat16)
        return high, low

    def one_block(row, slot):
        def param(k):
            return prep[k, pl.ds(row, 1), :]

        h2 = param(4)
        across = bump(param(0), param(1), h2)
        down = bump(param(2), param(3), h2)
        spread = jnp.concatenate([across * param(5 + c) for c in range(4)], axis=0)
        lhs = jnp.concatenate(split(spread), axis=1)
        y_high, y_low = split(down)
        rhs = jnp.concatenate(
            [jnp.concatenate([y_high, y_high], axis=1), jnp.concatenate([y_low, y_low], axis=1)],
            axis=0)
        res = lax.dot_general(lhs, rhs, (((1,), (1,)), ((), ())),
                              preferred_element_type=jnp.float32)
        return res

    def one_chunk(chunk, carry):
        for copy in copies(chunk):
            copy.wait()
        first = pl.multiple_of(chunk * rows, rows)

        @pl.when(first < live_count)
        def _():
            sl = pl.ds(first, rows)
            for axis in range(2):
                edge = corner_v[axis, sl].astype(jnp.float32)
                prep[2 * axis] = edge
                prep[2 * axis + 1] = edge + float(FOOT) * offset_v[axis, sl] - 0.5
            h2 = radius_v[sl] * radius_v[sl]
            prep[4] = h2
            inv = 1.0 / h2
            inv = inv * inv
            slot_index = first + lax.broadcasted_iota(jnp.int32, (rows, pb), 0)
            scale = jnp.where(slot_index < live_count, inv * inv, 0.0)
            for c in range(3):
                prep[5 + c] = emission_v[c, sl] * scale
            prep[8] = extinction_v[sl] * scale
            live_here = jnp.minimum(live_count - first, rows)

            def one_group(group, inner):
                base = group * UNROLL
                results = [one_block(base + k, first + base + k) for k in range(UNROLL)]
                for k in range(UNROLL):
                    t = tile_ref[0, first + base + k]
                    acc[t] = acc[t] + results[k]
                return inner

            lax.fori_loop(0, (live_here + UNROLL - 1) // UNROLL, one_group, 0)

        return carry

    lax.fori_loop(0, N_CHUNK, one_chunk, 0)

    def finish(group, carry):
        pieces = []
        for q in range(TILE_DEV):
            tile = acc[group * TILE_DEV + q]
            pieces.append(tile[:, :TS] + tile[:, TS:])
        out_ref[group] = jnp.concatenate(pieces, axis=1)
        return carry

    lax.fori_loop(0, tiles_all // TILE_DEV, finish, 0)


def deposit(block_tile, block_count, corner, offset, radius, emission, extinction, tiles_all):
    slots, pb = radius.shape[1:]
    any_space = pl.BlockSpec(memory_space=pl.ANY)
    smem = pl.BlockSpec(memory_space=pltpu.SMEM)
    return pl.pallas_call(
        functools.partial(deposit_kernel, tiles_all, slots, pb),
        out_shape=jax.ShapeDtypeStruct((tiles_all // TILE_DEV, 4 * TS, TILE_DEV * TS), jnp.float32),
        in_specs=[smem, smem] + [any_space] * 5,
        out_specs=pl.BlockSpec(memory_space=pltpu.VMEM),
        scratch_shapes=[
            pltpu.VMEM((2, slots, pb), jnp.int32),
            pltpu.VMEM((2, slots, pb), jnp.float32),
            pltpu.VMEM((slots, pb), jnp.float32),
            pltpu.VMEM((3, slots, pb), jnp.float32),
            pltpu.VMEM((slots, pb), jnp.float32),
            pltpu.VMEM((9, slots // N_CHUNK, pb), jnp.float32),
            pltpu.VMEM((tiles_all, 4 * TS, 2 * TS), jnp.float32),
            pltpu.SemaphoreType.DMA((N_CHUNK, 5)),
        ],
        compiler_params=pltpu.CompilerParams(vmem_limit_bytes=60 * 1024 * 1024),
        name="deposit",
    )(block_count, block_tile, corner, offset, radius, emission, extinction)


def composite(stacked, slab_rank):
    slabs = stacked.shape[0]
    optical = stacked[:, 3 * TS:]
    glow = stacked[:, :3 * TS].reshape(slabs, 3, TS, TILE_DEV * TS)
    before = (slab_rank[None, :] < slab_rank[:, None]).astype(jnp.float32)
    prior = sum(before[:, k, None, None] * optical[k][None] for k in range(slabs))
    fade = jnp.exp(-prior) * jnp.exp(-0.5 * optical)
    light = jnp.sum(fade[:, None] * glow, axis=0).reshape(3 * TS, TILE_DEV * TS)
    cover = 1.0 - jnp.exp(-jnp.sum(optical, axis=0))
    image = jnp.concatenate([light, cover], axis=0)
    return image.reshape(4 * TS, TILE_DEV, TS).transpose(1, 2, 0)


def shards(block_tile, block_count, slab_rank, corner, offset, radius, emission, extinction):
    depth_size = lax.axis_size("depth")
    screen_size = lax.axis_size("screen")
    tiles_all = TILE_DEV * depth_size * screen_size
    partial = deposit(block_tile, block_count, corner, offset, radius, emission, extinction, tiles_all)
    shaped = partial.reshape(depth_size, screen_size, 4 * TS, TILE_DEV * TS)
    owned = lax.psum_scatter(shaped, "screen", scatter_dimension=1, tiled=True)
    owned = owned.reshape(depth_size, 4 * TS, TILE_DEV * TS)
    slabs = lax.all_to_all(owned, "depth", split_axis=0, concat_axis=0, tiled=True)
    return composite(slabs, slab_rank)


def solution(mesh):
    placed = (
        P("depth", "screen"),
        P("depth", "screen"),
        P(),
        P(None, "depth", "screen", None),
        P(None, "depth", "screen", None),
        P("depth", "screen", None),
        P(None, "depth", "screen", None),
        P("depth", "screen", None),
    )
    return jax.shard_map(
        shards,
        mesh=mesh,
        in_specs=placed,
        out_specs=P(("depth", "screen"), None, None),
        check_vma=False,
    )
```

time: 1160 us -> 189 us (0.16)
  waiting for transfers between devices: 602 us -> 131 us
  matrix products: 318 us -> 0 us
  other arithmetic: 114 us -> 1.01 us
  local copies, waits for them, and re-layouts: 92.9 us -> 3.92 us
  Pallas kernels: 0 us -> 34.5 us
  blocking collectives: 13.2 us -> 0 us
    unnamed x2, waiting for transfers between devices: 602 us -> 121 us
    dot_general x5 -> x0, matrix products: 318 us -> none  [the longest x4 317 us: deposit(): jnp.einsum('gpy,cgpx->gycx', down_weights, spread, precision=lax.Precisio...]
    scatter-add x4 -> x0, other arithmetic: 89.7 us -> none  [one_round(): return tile_sums.at[ids_now].add(deposit_out)]
    dot_general x4 -> x0, local copies, waits for them, and re-layouts: 53.2 us -> none  [deposit(): jnp.einsum('gpy,cgpx->gycx', down_weights, spread, precision=lax.Precisio...]
    pallas_call x0 -> x1, Pallas kernels: none -> 34.5 us  [deposit(): pl.pallas_call(functools.partial(deposit_kernel, tiles_all, slots, pb), o...]
    reshape x6 -> x1, local copies, waits for them, and re-layouts: 23.7 us -> 2.52 us  [shards(): owned = owned.reshape(depth_size, 4 * TS, TILE_DEV * TS)]
    all_to_all x1 -> x0, blocking collectives: 13.2 us -> none  [shards(): lax.all_to_all(owned, 'depth', split_axis=0, concat_axis=0, tiled=True)]
  transfers between devices with their start and end apart: 1 -> 2, of which waited for: 1 -> 2; matrix products, arithmetic and copies ran while one was open for 0% -> 0% of each run, Pallas kernels for 0% -> 0%
where the time goes in v1:
time: 189 us; the launch traced here: 188 us
  waiting for transfers between devices  131 us (69%)
  Pallas kernels  34.5 us (18%)
  between operations  14.1 us (7%)
  local copies, waits for them, and re-layouts  3.92 us (2%)
  starting transfers between devices  3.66 us (2%)
    unnamed x2, waiting for transfers between devices  121 us
    pallas_call x1, Pallas kernels, deposit(): pl.pallas_call(functools.partial(deposit_kernel, tiles_all, slots, pb), o...  34.5 us
    all_to_all x1, waiting for transfers between devices, shards(): lax.all_to_all(owned, 'depth', split_axis=0, concat_axis=0, tiled=True)  9.63 us
  transfers between devices with their start and end apart: 2, of which 2 were waited for; matrix products, arithmetic and copies ran while one was open for 0% of the time, Pallas kernels for 0%

profile of v1, /device:TPU:0, one launch (start us, length us, event | category | flops | bytes accessed | tf_op | source)
XLA Modules:
  0.0 188.3 jit_solution(5615418190649716000)
XLA Ops:
  6.5 0.0 all-reduce.3.cloned.1.call-start
  7.2 34.5 %deposit.1 = f32[32,128,128]{2,1,0:T(8,128)} custom-call(s32[1,1]{1,0:T(1,128)S(6)} %copy.17.count_ref, s32[1,2048]{1,0:T(1,128)} %tile_ref.1, s32[2,1,2048,128]{3,2,1,0:T(8,128)} %corner_hbm.1, f32[2,1,2048,128]{3,2,1,0:T(8,128)} %offset_hbm.1, f32[1,2048,128]{2,1,0:T(8,128)} %radius_hbm.1, f32[3,1,2048,128]{3,2,1,0:T(8,128)} %emission_hbm.1, ...), custom_call_target="tpu_custom_call" | custom-call | tf_op jit(solution)/shard_map/deposit/pallas_call | solution.py:132
  41.7 0.0 copy-start.1
  41.7 0.0 copy-start
  41.8 0.0 all-reduce.3.cloned.1.call-update
  41.8 0.6 copy-done.1
  42.4 0.6 dynamic-slice
  43.0 121.4 %all-reduce.3.cloned.1.call-done = f32[8,4,128,128]{3,2,1,0:T(8,128)} async-done(((f32[8,4,128,128]{3,2,1,0:T(8,128)}), f32[8,4,128,128]{3,2,1,0:T(8,128)}) %all-reduce.3.cloned.1.call-update) | async-done | bytes 2097168
  164.4 2.5 %dynamic-slice_bitcast_fusion = f32[8,128,128]{2,1,0:T(8,128)} fusion(f32[8,4,128,128]{3,2,1,0:T(8,128)} %all-reduce.3.cloned.1.call-done, u32[]{:T(128)} %bitcast.8), kind=kLoop, calls=%fused_computation | loop fusion | bytes 1048580 | tf_op jit(solution)/shard_map/reshape | solution.py:172
  166.9 3.7 %all-to-all-start = ((f32[8,128,128]{2,1,0:T(8,128)}), f32[8,128,128]{2,1,0:T(8,128)S(1)}, u32[]{:S(2)}, u32[]{:S(2)}) async-start(f32[8,128,128]{2,1,0:T(8,128)} %dynamic-slice_bitcast_fusion), calls=%async_computation | async-start | bytes 1048576 | tf_op jit(solution)/shard_map/all_to_all | solution.py:173
  170.6 0.0 copy-done
  170.6 0.1 compare_convert_fusion
  170.7 9.6 %all-to-all-done = f32[8,128,128]{2,1,0:T(8,128)S(1)} async-done(((f32[8,128,128]{2,1,0:T(8,128)}), f32[8,128,128]{2,1,0:T(8,128)S(1)}, u32[]{:S(2)}, u32[]{:S(2)}) %all-to-all-start) | async-done | bytes 524320 | tf_op jit(solution)/shard_map/all_to_all | solution.py:173
  180.3 0.2 exponential_multiply_fusion
  180.5 0.1 copy.11
  180.6 0.1 copy.15
  180.7 0.7 maximum_bitcast_fusion
  (4 shorter events, 0.1 us)
Async XLA Ops:
  6.5 157.9 %all-reduce.3.cloned.1.call-start = ((), (), s32[]{:S(2)}) async-start(), calls=%async_computation.1 | async-start | bytes 4194304
  41.7 0.7 copy-start.1
  41.7 128.8 %copy-start = (s32[8]{0:T(128)S(1)}, s32[8]{0:T(128)}, u32[]{:S(2)}) copy-start(s32[8]{0:T(128)} %param.10) | copy-start | bytes 100
  166.9 13.4 %all-to-all-start = ((f32[8,128,128]{2,1,0:T(8,128)}), f32[8,128,128]{2,1,0:T(8,128)S(1)}, u32[]{:S(2)}, u32[]{:S(2)}) async-start(f32[8,128,128]{2,1,0:T(8,128)} %dynamic-slice_bitcast_fusion), calls=%async_computation | async-start | bytes 1048576 | tf_op jit(solution)/shard_map/all_to_all | solution.py:173
Sparse Core Ops, SparseCore 0:
  41.9 122.4 all-reduce.2

commit v2 on v1

--- a/solution.py
+++ b/solution.py
@@ -11,12 +11,15 @@
 FOOT = 16
 TILE_DEV = 4
 N_CHUNK = 16
-UNROLL = 16
-
-
-def deposit_kernel(tiles_all, slots, pb, count_ref, tile_ref, corner_hbm, offset_hbm, radius_hbm,
-                   emission_hbm, extinction_hbm, out_ref,
-                   corner_v, offset_v, radius_v, emission_v, extinction_v, prep, acc, sems):
+UNROLL = 128
+SKEW = 4
+
+
+def deposit_kernel(tiles_all, slots, pb, screen_size, count_ref, place_ref, tile_ref, corner_hbm,
+                   offset_hbm, radius_hbm, emission_hbm, extinction_hbm, *rest):
+    outs = rest[:screen_size]
+    (corner_v, offset_v, radius_v, emission_v, extinction_v, prep, acc,
+     late_lhs, late_rhs, sems) = rest[screen_size:]
     rows = slots // N_CHUNK
     live_count = count_ref[0, 0]
 
@@ -35,7 +38,7 @@
             copy.start()
         return carry
 
-    lax.fori_loop(0, N_CHUNK, start_chunk, 0)
+    lax.fori_loop(0, 2, start_chunk, 0)
 
     def clear(t, carry):
         acc[t] = jnp.zeros((4 * TS, 2 * TS), jnp.float32)
@@ -55,12 +58,10 @@
         p = jnp.maximum(jnp.where(inside, p, 0.0), 0.0)
         return p * p
 
-    def split(value):
-        high = value.astype(jnp.bfloat16)
-        low = (value - high.astype(jnp.float32)).astype(jnp.bfloat16)
-        return high, low
-
-    def one_block(row, slot):
+    def with_rest(value):
+        return value, value - value.astype(jnp.bfloat16).astype(jnp.float32)
+
+    def factors(row):
         def param(k):
             return prep[k, pl.ds(row, 1), :]
 
@@ -68,18 +69,32 @@
         across = bump(param(0), param(1), h2)
         down = bump(param(2), param(3), h2)
         spread = jnp.concatenate([across * param(5 + c) for c in range(4)], axis=0)
-        lhs = jnp.concatenate(split(spread), axis=1)
-        y_high, y_low = split(down)
+        lhs = jnp.concatenate(with_rest(spread), axis=1)
         rhs = jnp.concatenate(
-            [jnp.concatenate([y_high, y_high], axis=1), jnp.concatenate([y_low, y_low], axis=1)],
-            axis=0)
-        res = lax.dot_general(lhs, rhs, (((1,), (1,)), ((), ())),
-                              preferred_element_type=jnp.float32)
-        return res
+            [jnp.concatenate([part, part], axis=1) for part in with_rest(down)], axis=0)
+        return lhs, rhs
+
+    def product(lhs, rhs):
+        return lax.dot_general(lhs, rhs, (((1,), (1,)), ((), ())),
+                               preferred_element_type=jnp.float32)
+
+    def add_late(base):
+        for k in range(SKEW):
+            t = tile_ref[0, jnp.maximum(base - SKEW + k, 0)]
+            acc[t] = acc[t] + product(late_lhs[k], late_rhs[k])
+
+    for k in range(SKEW):
+        late_lhs[k] = jnp.zeros(late_lhs.shape[1:], jnp.float32)
+        late_rhs[k] = jnp.zeros(late_rhs.shape[1:], jnp.float32)
 
     def one_chunk(chunk, carry):
         for copy in copies(chunk):
             copy.wait()
+
+        @pl.when(chunk + 2 < N_CHUNK)
+        def _():
+            start_chunk(chunk + 2, 0)
+
         first = pl.multiple_of(chunk * rows, rows)
 
         @pl.when(first < live_count)
@@ -102,10 +117,14 @@
 
             def one_group(group, inner):
                 base = group * UNROLL
-                results = [one_block(base + k, first + base + k) for k in range(UNROLL)]
-                for k in range(UNROLL):
-                    t = tile_ref[0, first + base + k]
-                    acc[t] = acc[t] + results[k]
+                late = [product(late_lhs[k], late_rhs[k]) for k in range(SKEW)]
+                pairs = [factors(base + k) for k in range(UNROLL)]
+                results = [product(*pair) for pair in pairs[:UNROLL - SKEW]]
+                for k in range(SKEW):
+                    late_lhs[k], late_rhs[k] = pairs[UNROLL - SKEW + k]
+                for k, res in enumerate(late + results):
+                    t = tile_ref[0, jnp.maximum(first + base - SKEW + k, 0)]
+                    acc[t] = acc[t] + res
                 return inner
 
             lax.fori_loop(0, (live_here + UNROLL - 1) // UNROLL, one_group, 0)
@@ -114,26 +133,35 @@
 
     lax.fori_loop(0, N_CHUNK, one_chunk, 0)
 
-    def finish(group, carry):
-        pieces = []
-        for q in range(TILE_DEV):
-            tile = acc[group * TILE_DEV + q]
-            pieces.append(tile[:, :TS] + tile[:, TS:])
-        out_ref[group] = jnp.concatenate(pieces, axis=1)
-        return carry
-
-    lax.fori_loop(0, tiles_all // TILE_DEV, finish, 0)
-
-
-def deposit(block_tile, block_count, corner, offset, radius, emission, extinction, tiles_all):
+    add_late((live_count + UNROLL - 1) // UNROLL * UNROLL)
+
+    lane = lax.broadcasted_iota(jnp.int32, (4 * TS, TILE_DEV * TS), 1)
+    even = (lane // TS) % 2 == 0
+
+    def finish(d, carry):
+        for k in range(screen_size):
+            s = lax.rem(place_ref[0, 0] + k, screen_size)
+            tile = (d * screen_size + s) * TILE_DEV
+            wide = [jnp.concatenate([acc[tile + q], acc[tile + q + 2]], axis=1) for q in range(2)]
+            turned = [pltpu.roll(wide[0], 3 * TS, axis=1), pltpu.roll(wide[1], TS, axis=1)]
+            outs[k][d] = jnp.where(even, wide[0] + turned[0], wide[1] + turned[1])
+        return carry
+
+    lax.fori_loop(0, tiles_all // (TILE_DEV * screen_size), finish, 0)
+
+
+def deposit(block_tile, block_count, corner, offset, radius, emission, extinction, tiles_all,
+            place, screen_size):
     slots, pb = radius.shape[1:]
     any_space = pl.BlockSpec(memory_space=pl.ANY)
     smem = pl.BlockSpec(memory_space=pltpu.SMEM)
     return pl.pallas_call(
-        functools.partial(deposit_kernel, tiles_all, slots, pb),
-        out_shape=jax.ShapeDtypeStruct((tiles_all // TILE_DEV, 4 * TS, TILE_DEV * TS), jnp.float32),
-        in_specs=[smem, smem] + [any_space] * 5,
-        out_specs=pl.BlockSpec(memory_space=pltpu.VMEM),
+        functools.partial(deposit_kernel, tiles_all, slots, pb, screen_size),
+        out_shape=[jax.ShapeDtypeStruct(
+            (tiles_all // (TILE_DEV * screen_size), 4 * TS, TILE_DEV * TS), jnp.float32)
+        ] * screen_size,
+        in_specs=[smem, smem, smem] + [any_space] * 5,
+        out_specs=[pl.BlockSpec(memory_space=pltpu.VMEM)] * screen_size,
         scratch_shapes=[
             pltpu.VMEM((2, slots, pb), jnp.int32),
             pltpu.VMEM((2, slots, pb), jnp.float32),
@@ -142,11 +170,13 @@
             pltpu.VMEM((slots, pb), jnp.float32),
             pltpu.VMEM((9, slots // N_CHUNK, pb), jnp.float32),
             pltpu.VMEM((tiles_all, 4 * TS, 2 * TS), jnp.float32),
+            pltpu.VMEM((SKEW, 4 * TS, 2 * pb), jnp.float32),
+            pltpu.VMEM((SKEW, 2 * TS, 2 * pb), jnp.float32),
             pltpu.SemaphoreType.DMA((N_CHUNK, 5)),
         ],
         compiler_params=pltpu.CompilerParams(vmem_limit_bytes=60 * 1024 * 1024),
         name="deposit",
-    )(block_count, block_tile, corner, offset, radius, emission, extinction)
+    )(block_count, place, block_tile, corner, offset, radius, emission, extinction)
 
 
 def composite(stacked, slab_rank):
@@ -166,11 +196,23 @@
     depth_size = lax.axis_size("depth")
     screen_size = lax.axis_size("screen")
     tiles_all = TILE_DEV * depth_size * screen_size
-    partial = deposit(block_tile, block_count, corner, offset, radius, emission, extinction, tiles_all)
-    shaped = partial.reshape(depth_size, screen_size, 4 * TS, TILE_DEV * TS)
-    owned = lax.psum_scatter(shaped, "screen", scatter_dimension=1, tiled=True)
-    owned = owned.reshape(depth_size, 4 * TS, TILE_DEV * TS)
-    slabs = lax.all_to_all(owned, "depth", split_axis=0, concat_axis=0, tiled=True)
+    me = lax.axis_index("screen")
+    partial = deposit(block_tile, block_count, corner, offset, radius, emission, extinction,
+                      tiles_all, me.astype(jnp.int32).reshape(1, 1), screen_size)
+    owned = partial[0]
+    moved = [
+        lax.ppermute(partial[k], "screen", [(i, (i + k) % screen_size) for i in range(screen_size)])
+        for k in range(1, screen_size)
+    ]
+    for block in moved:
+        owned = owned + block
+    dme = lax.axis_index("depth")
+    pieces = [lax.dynamic_index_in_dim(owned, dme, 0, keepdims=True)]
+    for k in range(1, depth_size):
+        block = lax.dynamic_index_in_dim(owned, dme ^ k, 0, keepdims=True)
+        pieces.append(lax.ppermute(block, "depth", [(i, i ^ k) for i in range(depth_size)]))
+    slabs = jnp.concatenate(pieces, axis=0)
+    slab_rank = slab_rank[dme ^ jnp.arange(depth_size)]
     return composite(slabs, slab_rank)
 
 

time: 189 us -> 95.1 us (0.50)
  waiting for transfers between devices: 131 us -> 46.3 us
  starting transfers between devices: 3.66 us -> 21.9 us
  between operations: 14.1 us -> 0.82 us
  Pallas kernels: 34.5 us -> 22.5 us
  local copies, waits for them, and re-layouts: 3.92 us -> 0.96 us
    unnamed x2 -> x0, waiting for transfers between devices: 121 us -> none
    ppermute x0 -> x10, waiting for transfers between devices: none -> 46.3 us  [the longest x3 42.3 us: shards(): lax.ppermute(partial[k], 'screen', [(i, (i + k) % screen_size) for i in r...]
    ppermute x0 -> x10, starting transfers between devices: none -> 21.9 us  [the longest x3 13.5 us: shards(): lax.ppermute(partial[k], 'screen', [(i, (i + k) % screen_size) for i in r...]
    pallas_call x1, Pallas kernels: 34.5 us -> 22.5 us  [deposit(): pl.pallas_call(functools.partial(deposit_kernel, tiles_all, slots, pb, sc...]
    all_to_all x1 -> x0, waiting for transfers between devices: 9.63 us -> none  [shards(): lax.all_to_all(owned, 'depth', split_axis=0, concat_axis=0, tiled=True)]
    all_to_all x1 -> x0, starting transfers between devices: 3.65 us -> none  [shards(): lax.all_to_all(owned, 'depth', split_axis=0, concat_axis=0, tiled=True)]
    reshape x1 -> x0, local copies, waits for them, and re-layouts: 2.52 us -> none  [shards(): owned = owned.reshape(depth_size, 4 * TS, TILE_DEV * TS)]
  transfers between devices with their start and end apart: 2 -> 10, of which waited for: 2 -> 5; matrix products, arithmetic and copies ran while one was open for 0% -> 1% of each run, Pallas kernels for 0% -> 0%
where the time goes in v2:
time: 95.1 us; the launch traced here: 94.7 us
  waiting for transfers between devices  46.3 us (49%)
  Pallas kernels  22.5 us (24%)
  starting transfers between devices  21.9 us (23%)
  other arithmetic  2.2 us (2%)
  local copies, waits for them, and re-layouts  0.96 us (1%)
    ppermute x3, waiting for transfers between devices, shards(): lax.ppermute(partial[k], 'screen', [(i, (i + k) % screen_size) for i in r...  42.3 us
    pallas_call x1, Pallas kernels, deposit(): pl.pallas_call(functools.partial(deposit_kernel, tiles_all, slots, pb, sc...  22.5 us
    ppermute x3, starting transfers between devices, shards(): lax.ppermute(partial[k], 'screen', [(i, (i + k) % screen_size) for i in r...  13.5 us
    ppermute x7, starting transfers between devices, shards(): lax.ppermute(block, 'depth', [(i, i ^ k) for i in range(depth_size)])  8.49 us
    ppermute x7, waiting for transfers between devices, shards(): lax.ppermute(block, 'depth', [(i, i ^ k) for i in range(depth_size)])  4.05 us
  transfers between devices with their start and end apart: 10, of which 5 were waited for; matrix products, arithmetic and copies ran while one was open for 1% of the time, Pallas kernels for 0%

profile of v2, /device:TPU:0, one launch (start us, length us, event | category | flops | bytes accessed | tf_op | source)
XLA Modules:
  0.0 94.7 jit_solution(87009881081439512)
XLA Ops:
  0.7 22.5 %deposit.1 = (f32[8,128,128]{2,1,0:T(8,128)}, f32[8,128,128]{2,1,0:T(8,128)}, f32[8,128,128]{2,1,0:T(8,128)}, f32[8,128,128]{2,1,0:T(8,128)}) custom-call(s32[1,1]{1,0:T(1,128)S(6)} %copy.21.count_ref, s32[1,1]{1,0:T(1,128)} %bitcast.2.place_ref, s32[1,2048]{1,0:T(1,128)} %tile_ref.1, s32[2,1,2048,128]{3,2,1,0:T(8,128)} %corner_hbm.1, ...), custom_call_target="tpu_custom_call" | custom-call | tf_op jit(solution)/shard_map/deposit/pallas_call | solution.py:158
  23.2 7.0 %collective-permute-start.2 = (f32[8,128,128]{2,1,0:T(8,128)}, f32[8,128,128]{2,1,0:T(8,128)S(1)}, u32[]{:S(2)}, u32[]{:S(2)}) collective-permute-start(f32[8,128,128]{2,1,0:T(8,128)} %get-tuple-element.12), channel_id=1, source_target_pairs={{0,3},{1,0},{2,1},{3,2},{4,7},{5,4},{6,5},{7,6},{8,11},{9,8},{10,9... | collective-permute-start | bytes 1572872 | tf_op jit(solution)/shard_map/ppermute | solution.py:204
  30.2 6.4 %collective-permute-start.1 = (f32[8,128,128]{2,1,0:T(8,128)}, f32[8,128,128]{2,1,0:T(8,128)S(1)}, u32[]{:S(2)}, u32[]{:S(2)}) collective-permute-start(f32[8,128,128]{2,1,0:T(8,128)} %get-tuple-element.11), channel_id=1, source_target_pairs={{0,2},{1,3},{2,0},{3,1},{4,6},{5,7},{6,4},{7,5},{8,10},{9,11},{10,... | collective-permute-start | bytes 1572872 | tf_op jit(solution)/shard_map/ppermute | solution.py:204
  36.6 0.6 gather_fusion
  37.3 0.1 compare_convert_fusion
  37.4 7.6 %collective-permute-done.2 = f32[8,128,128]{2,1,0:T(8,128)S(1)} collective-permute-done((f32[8,128,128]{2,1,0:T(8,128)}, f32[8,128,128]{2,1,0:T(8,128)S(1)}, u32[]{:S(2)}, u32[]{:S(2)}) %collective-permute-start.2) | collective-permute-done | bytes 524320 | tf_op jit(solution)/shard_map/ppermute | solution.py:204
  44.9 34.7 %collective-permute-done.1 = f32[8,128,128]{2,1,0:T(8,128)S(1)} collective-permute-done((f32[8,128,128]{2,1,0:T(8,128)}, f32[8,128,128]{2,1,0:T(8,128)S(1)}, u32[]{:S(2)}, u32[]{:S(2)}) %collective-permute-start.1) | collective-permute-done | bytes 524320 | tf_op jit(solution)/shard_map/ppermute | solution.py:204
  79.6 1.2 %add_add_fusion = f32[8,128,128]{2,1,0:T(8,128)S(1)} fusion(f32[8,128,128]{2,1,0:T(8,128)S(1)} %collective-permute-done.2, f32[8,128,128]{2,1,0:T(8,128)S(1)} %collective-permute-done.1, f32[8,128,128]{2,1,0:T(8,128)} %get-tuple-element.9, f32[8,128,128]{2,1,0:T(8,128)S(1)} %collective-permute-done), kind=kLoop, calls=%fused_computation.1 | loop fusion | flops 393216 | bytes 2621440 | tf_op jit(solution)/shard_map/add | solution.py:208
  80.8 0.1 constant_dynamic-slice_fusion
  80.9 0.1 collective-permute-start.3
  81.0 3.9 %collective-permute-start.4 = (f32[1,128,128]{2,1,0:T(8,128)S(1)}, f32[1,128,128]{2,1,0:T(8,128)S(1)}, u32[]{:S(2)}, u32[]{:S(2)}) collective-permute-start(f32[1,128,128]{2,1,0:T(8,128)S(1)} %get-tuple-element.20), channel_id=1, source_target_pairs={{0,8},{4,12},{8,0},{12,4},{16,24},{20,28},{24,16},{28,20},{1,9},{5... | collective-permute-start | bytes 196616 | tf_op jit(solution)/shard_map/ppermute | solution.py:213
  84.9 0.0 collective-permute-start.5
  84.9 0.0 collective-permute-start.6
  84.9 1.5 %collective-permute-start.7 = (f32[1,128,128]{2,1,0:T(8,128)S(1)}, f32[1,128,128]{2,1,0:T(8,128)S(1)}, u32[]{:S(2)}, u32[]{:S(2)}) collective-permute-start(f32[1,128,128]{2,1,0:T(8,128)S(1)} %get-tuple-element.17), channel_id=1, source_target_pairs={{0,20},{4,16},{8,28},{12,24},{16,4},{20,0},{24,12},{28,8},{1,21},{... | collective-permute-start | bytes 196616 | tf_op jit(solution)/shard_map/ppermute | solution.py:213
  86.4 1.8 %collective-permute-start.8 = (f32[1,128,128]{2,1,0:T(8,128)S(1)}, f32[1,128,128]{2,1,0:T(8,128)S(1)}, u32[]{:S(2)}, u32[]{:S(2)}) collective-permute-start(f32[1,128,128]{2,1,0:T(8,128)S(1)} %get-tuple-element.16), channel_id=1, source_target_pairs={{0,24},{4,28},{8,16},{12,20},{16,8},{20,12},{24,0},{28,4},{1,25},{... | collective-permute-start | bytes 196616 | tf_op jit(solution)/shard_map/ppermute | solution.py:213
  88.2 0.0 collective-permute-done.4
  88.2 1.2 %collective-permute-start.9 = (f32[1,128,128]{2,1,0:T(8,128)S(1)}, f32[1,128,128]{2,1,0:T(8,128)S(1)}, u32[]{:S(2)}, u32[]{:S(2)}) collective-permute-start(f32[1,128,128]{2,1,0:T(8,128)S(1)} %get-tuple-element.15), channel_id=1, source_target_pairs={{0,28},{4,24},{8,20},{12,16},{16,12},{20,8},{24,4},{28,0},{1,29},{... | collective-permute-start | bytes 196616 | tf_op jit(solution)/shard_map/ppermute | solution.py:213
  89.5 0.3 collective-permute-done.6
  89.8 2.1 %collective-permute-done.8 = f32[1,128,128]{2,1,0:T(8,128)S(1)} collective-permute-done((f32[1,128,128]{2,1,0:T(8,128)S(1)}, f32[1,128,128]{2,1,0:T(8,128)S(1)}, u32[]{:S(2)}, u32[]{:S(2)}) %collective-permute-start.8) | collective-permute-done | bytes 65568 | tf_op jit(solution)/shard_map/ppermute | solution.py:213
  92.0 1.6 %collective-permute-done.9 = f32[1,128,128]{2,1,0:T(8,128)S(1)} collective-permute-done((f32[1,128,128]{2,1,0:T(8,128)S(1)}, f32[1,128,128]{2,1,0:T(8,128)S(1)}, u32[]{:S(2)}, u32[]{:S(2)}) %collective-permute-start.9) | collective-permute-done | bytes 65568 | tf_op jit(solution)/shard_map/ppermute | solution.py:213
  93.6 0.2 exponential_multiply_fusion
  93.8 0.1 copy.13
  93.9 0.1 copy.11
  94.0 0.7 maximum_bitcast_fusion
  (27 shorter events, 0.1 us)
Async XLA Ops:
  0.0 36.6 %copy-start = (s32[8]{0:T(128)S(1)}, s32[8]{0:T(128)}, u32[]{:S(2)}) copy-start(s32[8]{0:T(128)} %param.10) | copy-start | bytes 100
  23.2 21.8 %collective-permute-start.2 = (f32[8,128,128]{2,1,0:T(8,128)}, f32[8,128,128]{2,1,0:T(8,128)S(1)}, u32[]{:S(2)}, u32[]{:S(2)}) collective-permute-start(f32[8,128,128]{2,1,0:T(8,128)} %get-tuple-element.12), channel_id=1, source_target_pairs={{0,3},{1,0},{2,1},{3,2},{4,7},{5,4},{6,5},{7,6},{8,11},{9,8},{10,9... | collective-permute-start | bytes 1572872 | tf_op jit(solution)/shard_map/ppermute | solution.py:204
  30.2 49.4 %collective-permute-start.1 = (f32[8,128,128]{2,1,0:T(8,128)}, f32[8,128,128]{2,1,0:T(8,128)S(1)}, u32[]{:S(2)}, u32[]{:S(2)}) collective-permute-start(f32[8,128,128]{2,1,0:T(8,128)} %get-tuple-element.11), channel_id=1, source_target_pairs={{0,2},{1,3},{2,0},{3,1},{4,6},{5,7},{6,4},{7,5},{8,10},{9,11},{10,... | collective-permute-start | bytes 1572872 | tf_op jit(solution)/shard_map/ppermute | solution.py:204
  36.6 43.0 %collective-permute-start = (f32[8,128,128]{2,1,0:T(8,128)}, f32[8,128,128]{2,1,0:T(8,128)S(1)}, u32[]{:S(2)}, u32[]{:S(2)}) collective-permute-start(f32[8,128,128]{2,1,0:T(8,128)} %get-tuple-element.10), channel_id=1, source_target_pairs={{0,1},{1,2},{2,3},{3,0},{4,5},{5,6},{6,7},{7,4},{8,9},{9,10},{10,1... | collective-permute-start | bytes 1572872 | tf_op jit(solution)/shard_map/ppermute | solution.py:204
  80.9 5.6 %collective-permute-start.3 = (f32[1,128,128]{2,1,0:T(8,128)S(1)}, f32[1,128,128]{2,1,0:T(8,128)S(1)}, u32[]{:S(2)}, u32[]{:S(2)}) collective-permute-start(f32[1,128,128]{2,1,0:T(8,128)S(1)} %get-tuple-element.21), channel_id=1, source_target_pairs={{0,4},{4,0},{8,12},{12,8},{16,20},{20,16},{24,28},{28,24},{1,5},{5... | collective-permute-start | bytes 196616 | tf_op jit(solution)/shard_map/ppermute | solution.py:213
  81.0 7.3 %collective-permute-start.4 = (f32[1,128,128]{2,1,0:T(8,128)S(1)}, f32[1,128,128]{2,1,0:T(8,128)S(1)}, u32[]{:S(2)}, u32[]{:S(2)}) collective-permute-start(f32[1,128,128]{2,1,0:T(8,128)S(1)} %get-tuple-element.20), channel_id=1, source_target_pairs={{0,8},{4,12},{8,0},{12,4},{16,24},{20,28},{24,16},{28,20},{1,9},{5... | collective-permute-start | bytes 196616 | tf_op jit(solution)/shard_map/ppermute | solution.py:213
  84.9 4.5 %collective-permute-start.5 = (f32[1,128,128]{2,1,0:T(8,128)S(1)}, f32[1,128,128]{2,1,0:T(8,128)S(1)}, u32[]{:S(2)}, u32[]{:S(2)}) collective-permute-start(f32[1,128,128]{2,1,0:T(8,128)S(1)} %get-tuple-element.19), channel_id=1, source_target_pairs={{0,12},{4,8},{8,4},{12,0},{16,28},{20,24},{24,20},{28,16},{1,13},{... | collective-permute-start | bytes 196616 | tf_op jit(solution)/shard_map/ppermute | solution.py:213
  84.9 4.9 %collective-permute-start.6 = (f32[1,128,128]{2,1,0:T(8,128)S(1)}, f32[1,128,128]{2,1,0:T(8,128)S(1)}, u32[]{:S(2)}, u32[]{:S(2)}) collective-permute-start(f32[1,128,128]{2,1,0:T(8,128)S(1)} %get-tuple-element.18), channel_id=1, source_target_pairs={{0,16},{4,20},{8,24},{12,28},{16,0},{20,4},{24,8},{28,12},{1,17},{... | collective-permute-start | bytes 196616 | tf_op jit(solution)/shard_map/ppermute | solution.py:213
  84.9 4.9 %collective-permute-start.7 = (f32[1,128,128]{2,1,0:T(8,128)S(1)}, f32[1,128,128]{2,1,0:T(8,128)S(1)}, u32[]{:S(2)}, u32[]{:S(2)}) collective-permute-start(f32[1,128,128]{2,1,0:T(8,128)S(1)} %get-tuple-element.17), channel_id=1, source_target_pairs={{0,20},{4,16},{8,28},{12,24},{16,4},{20,0},{24,12},{28,8},{1,21},{... | collective-permute-start | bytes 196616 | tf_op jit(solution)/shard_map/ppermute | solution.py:213
  86.4 5.5 %collective-permute-start.8 = (f32[1,128,128]{2,1,0:T(8,128)S(1)}, f32[1,128,128]{2,1,0:T(8,128)S(1)}, u32[]{:S(2)}, u32[]{:S(2)}) collective-permute-start(f32[1,128,128]{2,1,0:T(8,128)S(1)} %get-tuple-element.16), channel_id=1, source_target_pairs={{0,24},{4,28},{8,16},{12,20},{16,8},{20,12},{24,0},{28,4},{1,25},{... | collective-permute-start | bytes 196616 | tf_op jit(solution)/shard_map/ppermute | solution.py:213
  88.2 5.3 %collective-permute-start.9 = (f32[1,128,128]{2,1,0:T(8,128)S(1)}, f32[1,128,128]{2,1,0:T(8,128)S(1)}, u32[]{:S(2)}, u32[]{:S(2)}) collective-permute-start(f32[1,128,128]{2,1,0:T(8,128)S(1)} %get-tuple-element.15), channel_id=1, source_target_pairs={{0,28},{4,24},{8,20},{12,16},{16,12},{20,8},{24,4},{28,0},{1,29},{... | collective-permute-start | bytes 196616 | tf_op jit(solution)/shard_map/ppermute | solution.py:213

commit v3 on v2

--- a/solution.py
+++ b/solution.py
@@ -15,11 +15,11 @@
 SKEW = 4
 
 
-def deposit_kernel(tiles_all, slots, pb, screen_size, count_ref, place_ref, tile_ref, corner_hbm,
+def deposit_kernel(tiles_all, slots, pb, screen_size, count_ref, place_ref, tile_hbm, corner_hbm,
                    offset_hbm, radius_hbm, emission_hbm, extinction_hbm, *rest):
     outs = rest[:screen_size]
     (corner_v, offset_v, radius_v, emission_v, extinction_v, prep, acc,
-     late_lhs, late_rhs, sems) = rest[screen_size:]
+     late_lhs, late_rhs, tile_ref, ready, sems, tile_sem, out_sems) = rest[screen_size:]
     rows = slots // N_CHUNK
     live_count = count_ref[0, 0]
 
@@ -39,6 +39,8 @@
         return carry
 
     lax.fori_loop(0, 2, start_chunk, 0)
+    tile_copy = pltpu.make_async_copy(tile_hbm, tile_ref, tile_sem)
+    tile_copy.start()
 
     def clear(t, carry):
         acc[t] = jnp.zeros((4 * TS, 2 * TS), jnp.float32)
@@ -46,17 +48,21 @@
 
     lax.fori_loop(0, tiles_all, clear, 0)
 
-    pixel = lax.broadcasted_iota(jnp.int32, (TS, pb), 0).astype(jnp.float32)
-    half = FOOT
-    low_pixel = pixel[:half]
-    high_pixel = pixel[half:] - float(FOOT)
+    quarter = TS // 4
+    pixel = lax.broadcasted_iota(jnp.int32, (quarter, pb), 0).astype(jnp.float32)
+    second_quarter = (pixel + float(quarter)) / float(FOOT)
 
     def bump(edge, centre, h2):
-        s = pixel - centre
-        p = h2 - s * s
-        inside = jnp.concatenate([low_pixel >= edge, high_pixel < edge], axis=0)
-        p = jnp.maximum(jnp.where(inside, p, 0.0), 0.0)
-        return p * p
+        s = second_quarter - centre
+        p1 = h2 - s * s
+        shared = p1 - 0.25
+        p0 = shared + s
+        p2 = shared - s
+        p3 = (p2 - s) - 0.75
+        inside = (pixel >= edge, pixel + float(quarter) >= edge,
+                  pixel < edge, pixel + float(quarter) < edge)
+        parts = [jnp.maximum(jnp.where(ok, p, 0.0), 0.0) for ok, p in zip(inside, (p0, p1, p2, p3))]
+        return jnp.concatenate([p * p for p in parts], axis=0)
 
     def with_rest(value):
         return value, value - value.astype(jnp.bfloat16).astype(jnp.float32)
@@ -87,6 +93,8 @@
         late_lhs[k] = jnp.zeros(late_lhs.shape[1:], jnp.float32)
         late_rhs[k] = jnp.zeros(late_rhs.shape[1:], jnp.float32)
 
+    tile_copy.wait()
+
     def one_chunk(chunk, carry):
         for copy in copies(chunk):
             copy.wait()
@@ -103,8 +111,9 @@
             for axis in range(2):
                 edge = corner_v[axis, sl].astype(jnp.float32)
                 prep[2 * axis] = edge
-                prep[2 * axis + 1] = edge + float(FOOT) * offset_v[axis, sl] - 0.5
-            h2 = radius_v[sl] * radius_v[sl]
+                prep[2 * axis + 1] = (edge - 0.5) / float(FOOT) + offset_v[axis, sl]
+            unit_radius = radius_v[sl] / float(FOOT)
+            h2 = unit_radius * unit_radius
             prep[4] = h2
             inv = 1.0 / h2
             inv = inv * inv
@@ -138,16 +147,27 @@
     lane = lax.broadcasted_iota(jnp.int32, (4 * TS, TILE_DEV * TS), 1)
     even = (lane // TS) % 2 == 0
 
+    def out_copy(k, d):
+        return pltpu.make_async_copy(ready.at[k, d], outs[k].at[d], out_sems.at[k, d])
+
     def finish(d, carry):
         for k in range(screen_size):
             s = lax.rem(place_ref[0, 0] + k, screen_size)
             tile = (d * screen_size + s) * TILE_DEV
             wide = [jnp.concatenate([acc[tile + q], acc[tile + q + 2]], axis=1) for q in range(2)]
             turned = [pltpu.roll(wide[0], 3 * TS, axis=1), pltpu.roll(wide[1], TS, axis=1)]
-            outs[k][d] = jnp.where(even, wide[0] + turned[0], wide[1] + turned[1])
+            ready[k, d] = jnp.where(even, wide[0] + turned[0], wide[1] + turned[1])
+            out_copy(k, d).start()
         return carry
 
     lax.fori_loop(0, tiles_all // (TILE_DEV * screen_size), finish, 0)
+
+    def drain(d, carry):
+        for k in range(screen_size):
+            out_copy(k, d).wait()
+        return carry
+
+    lax.fori_loop(0, tiles_all // (TILE_DEV * screen_size), drain, 0)
 
 
 def deposit(block_tile, block_count, corner, offset, radius, emission, extinction, tiles_all,
@@ -160,8 +180,8 @@
         out_shape=[jax.ShapeDtypeStruct(
             (tiles_all // (TILE_DEV * screen_size), 4 * TS, TILE_DEV * TS), jnp.float32)
         ] * screen_size,
-        in_specs=[smem, smem, smem] + [any_space] * 5,
-        out_specs=[pl.BlockSpec(memory_space=pltpu.VMEM)] * screen_size,
+        in_specs=[smem, smem] + [any_space] * 6,
+        out_specs=[any_space] * screen_size,
         scratch_shapes=[
             pltpu.VMEM((2, slots, pb), jnp.int32),
             pltpu.VMEM((2, slots, pb), jnp.float32),
@@ -172,7 +192,12 @@
             pltpu.VMEM((tiles_all, 4 * TS, 2 * TS), jnp.float32),
             pltpu.VMEM((SKEW, 4 * TS, 2 * pb), jnp.float32),
             pltpu.VMEM((SKEW, 2 * TS, 2 * pb), jnp.float32),
+            pltpu.SMEM((1, slots), jnp.int32),
+            pltpu.VMEM((screen_size, tiles_all // (TILE_DEV * screen_size), 4 * TS, TILE_DEV * TS),
+                       jnp.float32),
             pltpu.SemaphoreType.DMA((N_CHUNK, 5)),
+            pltpu.SemaphoreType.DMA,
+            pltpu.SemaphoreType.DMA((screen_size, tiles_all // (TILE_DEV * screen_size))),
         ],
         compiler_params=pltpu.CompilerParams(vmem_limit_bytes=60 * 1024 * 1024),
         name="deposit",

time: 95.1 us -> 94.1 us (0.989); the launches traced: 94.7 us -> 96 us
  Pallas kernels: 22.5 us -> 25 us
  waiting for transfers between devices: 46.3 us -> 43.9 us
  starting transfers between devices: 21.9 us -> 23.1 us
    ppermute x7, starting transfers between devices: 8.49 us -> 17 us  [shards(): lax.ppermute(block, 'depth', [(i, i ^ k) for i in range(depth_size)])]
    ppermute x3, starting transfers between devices: 13.5 us -> 6.14 us  [shards(): lax.ppermute(partial[k], 'screen', [(i, (i + k) % screen_size) for i in r...]
    ppermute x3, waiting for transfers between devices: 42.3 us -> 38.7 us  [shards(): lax.ppermute(partial[k], 'screen', [(i, (i + k) % screen_size) for i in r...]
    pallas_call x1, Pallas kernels: 22.5 us -> 25 us  [deposit(): pl.pallas_call(functools.partial(deposit_kernel, tiles_all, slots, pb, sc...]
    ppermute x7, waiting for transfers between devices: 4.05 us -> 5.12 us  [shards(): lax.ppermute(block, 'depth', [(i, i ^ k) for i in range(depth_size)])]
  transfers between devices with their start and end apart: 10 -> 10, of which waited for: 5 -> 4; matrix products, arithmetic and copies ran while one was open for 1% -> 1% of each run, Pallas kernels for 0% -> 0%
where the time goes in v3:
time: 94.1 us; the launch traced here: 96 us
  waiting for transfers between devices  43.9 us (47%)
  Pallas kernels  25 us (27%)
  starting transfers between devices  23.1 us (25%)
  other arithmetic  2.2 us (2%)
  local copies, waits for them, and re-layouts  0.96 us (1%)
    ppermute x3, waiting for transfers between devices, shards(): lax.ppermute(partial[k], 'screen', [(i, (i + k) % screen_size) for i in r...  38.7 us
    pallas_call x1, Pallas kernels, deposit(): pl.pallas_call(functools.partial(deposit_kernel, tiles_all, slots, pb, sc...  25 us
    ppermute x7, starting transfers between devices, shards(): lax.ppermute(block, 'depth', [(i, i ^ k) for i in range(depth_size)])  17 us
    ppermute x3, starting transfers between devices, shards(): lax.ppermute(partial[k], 'screen', [(i, (i + k) % screen_size) for i in r...  6.14 us
    ppermute x7, waiting for transfers between devices, shards(): lax.ppermute(block, 'depth', [(i, i ^ k) for i in range(depth_size)])  5.12 us
  transfers between devices with their start and end apart: 10, of which 4 were waited for; matrix products, arithmetic and copies ran while one was open for 1% of the time, Pallas kernels for 0%

profile of v3, /device:TPU:0, one launch (start us, length us, event | category | flops | bytes accessed | tf_op | source)
XLA Modules:
  0.0 96.0 jit_solution(2368788097230690698)
XLA Ops:
  0.7 25.0 %deposit.1 = (f32[8,128,128]{2,1,0:T(8,128)}, f32[8,128,128]{2,1,0:T(8,128)}, f32[8,128,128]{2,1,0:T(8,128)}, f32[8,128,128]{2,1,0:T(8,128)}) custom-call(s32[1,1]{1,0:T(1,128)S(6)} %copy.21.count_ref, s32[1,1]{1,0:T(1,128)} %bitcast.2.place_ref, s32[1,2048]{1,0:T(1,128)} %tile_hbm.1, s32[2,1,2048,128]{3,2,1,0:T(8,128)} %corner_hbm.1, ...), custom_call_target="tpu_custom_call" | custom-call | tf_op jit(solution)/shard_map/deposit/pallas_call | solution.py:178
  25.7 2.8 %collective-permute-start.2 = (f32[8,128,128]{2,1,0:T(8,128)}, f32[8,128,128]{2,1,0:T(8,128)S(1)}, u32[]{:S(2)}, u32[]{:S(2)}) collective-permute-start(f32[8,128,128]{2,1,0:T(8,128)} %get-tuple-element.12), channel_id=1, source_target_pairs={{0,3},{1,0},{2,1},{3,2},{4,7},{5,4},{6,5},{7,6},{8,11},{9,8},{10,9... | collective-permute-start | bytes 1572872 | tf_op jit(solution)/shard_map/ppermute | solution.py:229
  28.4 1.4 %collective-permute-start.1 = (f32[8,128,128]{2,1,0:T(8,128)}, f32[8,128,128]{2,1,0:T(8,128)S(1)}, u32[]{:S(2)}, u32[]{:S(2)}) collective-permute-start(f32[8,128,128]{2,1,0:T(8,128)} %get-tuple-element.11), channel_id=1, source_target_pairs={{0,2},{1,3},{2,0},{3,1},{4,6},{5,7},{6,4},{7,5},{8,10},{9,11},{10,... | collective-permute-start | bytes 1572872 | tf_op jit(solution)/shard_map/ppermute | solution.py:229
  29.9 1.9 %collective-permute-start = (f32[8,128,128]{2,1,0:T(8,128)}, f32[8,128,128]{2,1,0:T(8,128)S(1)}, u32[]{:S(2)}, u32[]{:S(2)}) collective-permute-start(f32[8,128,128]{2,1,0:T(8,128)} %get-tuple-element.10), channel_id=1, source_target_pairs={{0,1},{1,2},{2,3},{3,0},{4,5},{5,6},{6,7},{7,4},{8,9},{9,10},{10,1... | collective-permute-start | bytes 1572872 | tf_op jit(solution)/shard_map/ppermute | solution.py:229
  31.8 0.6 gather_fusion
  32.5 0.1 compare_convert_fusion
  32.6 7.3 %collective-permute-done.2 = f32[8,128,128]{2,1,0:T(8,128)S(1)} collective-permute-done((f32[8,128,128]{2,1,0:T(8,128)}, f32[8,128,128]{2,1,0:T(8,128)S(1)}, u32[]{:S(2)}, u32[]{:S(2)}) %collective-permute-start.2) | collective-permute-done | bytes 524320 | tf_op jit(solution)/shard_map/ppermute | solution.py:229
  39.9 31.4 %collective-permute-done.1 = f32[8,128,128]{2,1,0:T(8,128)S(1)} collective-permute-done((f32[8,128,128]{2,1,0:T(8,128)}, f32[8,128,128]{2,1,0:T(8,128)S(1)}, u32[]{:S(2)}, u32[]{:S(2)}) %collective-permute-start.1) | collective-permute-done | bytes 524320 | tf_op jit(solution)/shard_map/ppermute | solution.py:229
  71.3 0.0 collective-permute-done
  71.3 1.2 %add_add_fusion = f32[8,128,128]{2,1,0:T(8,128)S(1)} fusion(f32[8,128,128]{2,1,0:T(8,128)S(1)} %collective-permute-done.2, f32[8,128,128]{2,1,0:T(8,128)S(1)} %collective-permute-done.1, f32[8,128,128]{2,1,0:T(8,128)} %get-tuple-element.9, f32[8,128,128]{2,1,0:T(8,128)S(1)} %collective-permute-done), kind=kLoop, calls=%fused_computation.1 | loop fusion | flops 393216 | bytes 2621440 | tf_op jit(solution)/shard_map/add | solution.py:233
  72.5 0.1 constant_dynamic-slice_fusion
  72.5 5.1 %collective-permute-start.3 = (f32[1,128,128]{2,1,0:T(8,128)S(1)}, f32[1,128,128]{2,1,0:T(8,128)S(1)}, u32[]{:S(2)}, u32[]{:S(2)}) collective-permute-start(f32[1,128,128]{2,1,0:T(8,128)S(1)} %get-tuple-element.21), channel_id=1, source_target_pairs={{0,4},{4,0},{8,12},{12,8},{16,20},{20,16},{24,28},{28,24},{1,5},{5... | collective-permute-start | bytes 196616 | tf_op jit(solution)/shard_map/ppermute | solution.py:238
  77.6 1.9 %collective-permute-start.4 = (f32[1,128,128]{2,1,0:T(8,128)S(1)}, f32[1,128,128]{2,1,0:T(8,128)S(1)}, u32[]{:S(2)}, u32[]{:S(2)}) collective-permute-start(f32[1,128,128]{2,1,0:T(8,128)S(1)} %get-tuple-element.20), channel_id=1, source_target_pairs={{0,8},{4,12},{8,0},{12,4},{16,24},{20,28},{24,16},{28,20},{1,9},{5... | collective-permute-start | bytes 196616 | tf_op jit(solution)/shard_map/ppermute | solution.py:238
  79.5 7.0 %collective-permute-start.6 = (f32[1,128,128]{2,1,0:T(8,128)S(1)}, f32[1,128,128]{2,1,0:T(8,128)S(1)}, u32[]{:S(2)}, u32[]{:S(2)}) collective-permute-start(f32[1,128,128]{2,1,0:T(8,128)S(1)} %get-tuple-element.18), channel_id=1, source_target_pairs={{0,16},{4,20},{8,24},{12,28},{16,0},{20,4},{24,8},{28,12},{1,17},{... | collective-permute-start | bytes 196616 | tf_op jit(solution)/shard_map/ppermute | solution.py:238
  86.5 0.0 collective-permute-done.3
  86.5 2.9 %collective-permute-start.8 = (f32[1,128,128]{2,1,0:T(8,128)S(1)}, f32[1,128,128]{2,1,0:T(8,128)S(1)}, u32[]{:S(2)}, u32[]{:S(2)}) collective-permute-start(f32[1,128,128]{2,1,0:T(8,128)S(1)} %get-tuple-element.16), channel_id=1, source_target_pairs={{0,24},{4,28},{8,16},{12,20},{16,8},{20,12},{24,0},{28,4},{1,25},{... | collective-permute-start | bytes 196616 | tf_op jit(solution)/shard_map/ppermute | solution.py:238
  89.5 0.0 collective-permute-done.4
  89.5 0.1 collective-permute-start.9
  89.7 2.6 %collective-permute-done.7 = f32[1,128,128]{2,1,0:T(8,128)S(1)} collective-permute-done((f32[1,128,128]{2,1,0:T(8,128)S(1)}, f32[1,128,128]{2,1,0:T(8,128)S(1)}, u32[]{:S(2)}, u32[]{:S(2)}) %collective-permute-start.7) | collective-permute-done | bytes 65568 | tf_op jit(solution)/shard_map/ppermute | solution.py:238
  92.3 2.5 %collective-permute-done.9 = f32[1,128,128]{2,1,0:T(8,128)S(1)} collective-permute-done((f32[1,128,128]{2,1,0:T(8,128)S(1)}, f32[1,128,128]{2,1,0:T(8,128)S(1)}, u32[]{:S(2)}, u32[]{:S(2)}) %collective-permute-start.9) | collective-permute-done | bytes 65568 | tf_op jit(solution)/shard_map/ppermute | solution.py:238
  94.8 0.2 exponential_multiply_fusion
  95.0 0.1 copy.13
  95.1 0.1 copy.11
  95.2 0.7 maximum_bitcast_fusion
  (27 shorter events, 0.2 us)
Async XLA Ops:
  0.0 31.8 %copy-start = (s32[8]{0:T(128)S(1)}, s32[8]{0:T(128)}, u32[]{:S(2)}) copy-start(s32[8]{0:T(128)} %param.10) | copy-start | bytes 100
  25.7 14.2 %collective-permute-start.2 = (f32[8,128,128]{2,1,0:T(8,128)}, f32[8,128,128]{2,1,0:T(8,128)S(1)}, u32[]{:S(2)}, u32[]{:S(2)}) collective-permute-start(f32[8,128,128]{2,1,0:T(8,128)} %get-tuple-element.12), channel_id=1, source_target_pairs={{0,3},{1,0},{2,1},{3,2},{4,7},{5,4},{6,5},{7,6},{8,11},{9,8},{10,9... | collective-permute-start | bytes 1572872 | tf_op jit(solution)/shard_map/ppermute | solution.py:229
  28.4 42.9 %collective-permute-start.1 = (f32[8,128,128]{2,1,0:T(8,128)}, f32[8,128,128]{2,1,0:T(8,128)S(1)}, u32[]{:S(2)}, u32[]{:S(2)}) collective-permute-start(f32[8,128,128]{2,1,0:T(8,128)} %get-tuple-element.11), channel_id=1, source_target_pairs={{0,2},{1,3},{2,0},{3,1},{4,6},{5,7},{6,4},{7,5},{8,10},{9,11},{10,... | collective-permute-start | bytes 1572872 | tf_op jit(solution)/shard_map/ppermute | solution.py:229
  29.9 41.4 %collective-permute-start = (f32[8,128,128]{2,1,0:T(8,128)}, f32[8,128,128]{2,1,0:T(8,128)S(1)}, u32[]{:S(2)}, u32[]{:S(2)}) collective-permute-start(f32[8,128,128]{2,1,0:T(8,128)} %get-tuple-element.10), channel_id=1, source_target_pairs={{0,1},{1,2},{2,3},{3,0},{4,5},{5,6},{6,7},{7,4},{8,9},{9,10},{10,1... | collective-permute-start | bytes 1572872 | tf_op jit(solution)/shard_map/ppermute | solution.py:229
  72.5 14.0 %collective-permute-start.3 = (f32[1,128,128]{2,1,0:T(8,128)S(1)}, f32[1,128,128]{2,1,0:T(8,128)S(1)}, u32[]{:S(2)}, u32[]{:S(2)}) collective-permute-start(f32[1,128,128]{2,1,0:T(8,128)S(1)} %get-tuple-element.21), channel_id=1, source_target_pairs={{0,4},{4,0},{8,12},{12,8},{16,20},{20,16},{24,28},{28,24},{1,5},{5... | collective-permute-start | bytes 196616 | tf_op jit(solution)/shard_map/ppermute | solution.py:238
  77.6 11.9 %collective-permute-start.4 = (f32[1,128,128]{2,1,0:T(8,128)S(1)}, f32[1,128,128]{2,1,0:T(8,128)S(1)}, u32[]{:S(2)}, u32[]{:S(2)}) collective-permute-start(f32[1,128,128]{2,1,0:T(8,128)S(1)} %get-tuple-element.20), channel_id=1, source_target_pairs={{0,8},{4,12},{8,0},{12,4},{16,24},{20,28},{24,16},{28,20},{1,9},{5... | collective-permute-start | bytes 196616 | tf_op jit(solution)/shard_map/ppermute | solution.py:238
  79.5 10.0 %collective-permute-start.5 = (f32[1,128,128]{2,1,0:T(8,128)S(1)}, f32[1,128,128]{2,1,0:T(8,128)S(1)}, u32[]{:S(2)}, u32[]{:S(2)}) collective-permute-start(f32[1,128,128]{2,1,0:T(8,128)S(1)} %get-tuple-element.19), channel_id=1, source_target_pairs={{0,12},{4,8},{8,4},{12,0},{16,28},{20,24},{24,20},{28,16},{1,13},{... | collective-permute-start | bytes 196616 | tf_op jit(solution)/shard_map/ppermute | solution.py:238
  79.5 10.1 %collective-permute-start.6 = (f32[1,128,128]{2,1,0:T(8,128)S(1)}, f32[1,128,128]{2,1,0:T(8,128)S(1)}, u32[]{:S(2)}, u32[]{:S(2)}) collective-permute-start(f32[1,128,128]{2,1,0:T(8,128)S(1)} %get-tuple-element.18), channel_id=1, source_target_pairs={{0,16},{4,20},{8,24},{12,28},{16,0},{20,4},{24,8},{28,12},{1,17},{... | collective-permute-start | bytes 196616 | tf_op jit(solution)/shard_map/ppermute | solution.py:238
  86.5 5.8 %collective-permute-start.7 = (f32[1,128,128]{2,1,0:T(8,128)S(1)}, f32[1,128,128]{2,1,0:T(8,128)S(1)}, u32[]{:S(2)}, u32[]{:S(2)}) collective-permute-start(f32[1,128,128]{2,1,0:T(8,128)S(1)} %get-tuple-element.17), channel_id=1, source_target_pairs={{0,20},{4,16},{8,28},{12,24},{16,4},{20,0},{24,12},{28,8},{1,21},{... | collective-permute-start | bytes 196616 | tf_op jit(solution)/shard_map/ppermute | solution.py:238
  86.5 5.8 %collective-permute-start.8 = (f32[1,128,128]{2,1,0:T(8,128)S(1)}, f32[1,128,128]{2,1,0:T(8,128)S(1)}, u32[]{:S(2)}, u32[]{:S(2)}) collective-permute-start(f32[1,128,128]{2,1,0:T(8,128)S(1)} %get-tuple-element.16), channel_id=1, source_target_pairs={{0,24},{4,28},{8,16},{12,20},{16,8},{20,12},{24,0},{28,4},{1,25},{... | collective-permute-start | bytes 196616 | tf_op jit(solution)/shard_map/ppermute | solution.py:238
  89.5 5.3 %collective-permute-start.9 = (f32[1,128,128]{2,1,0:T(8,128)S(1)}, f32[1,128,128]{2,1,0:T(8,128)S(1)}, u32[]{:S(2)}, u32[]{:S(2)}) collective-permute-start(f32[1,128,128]{2,1,0:T(8,128)S(1)} %get-tuple-element.15), channel_id=1, source_target_pairs={{0,28},{4,24},{8,20},{12,16},{16,12},{20,8},{24,4},{28,0},{1,29},{... | collective-permute-start | bytes 196616 | tf_op jit(solution)/shard_map/ppermute | solution.py:238

commit v4 on v3

--- a/solution.py
+++ b/solution.py
@@ -48,36 +48,34 @@
 
     lax.fori_loop(0, tiles_all, clear, 0)
 
-    quarter = TS // 4
-    pixel = lax.broadcasted_iota(jnp.int32, (quarter, pb), 0).astype(jnp.float32)
-    second_quarter = (pixel + float(quarter)) / float(FOOT)
+    pixel = lax.broadcasted_iota(jnp.int32, (FOOT, pb), 0).astype(jnp.float32)
+    unit = pixel / float(FOOT)
 
     def bump(edge, centre, h2):
-        s = second_quarter - centre
-        p1 = h2 - s * s
-        shared = p1 - 0.25
-        p0 = shared + s
-        p2 = shared - s
-        p3 = (p2 - s) - 0.75
-        inside = (pixel >= edge, pixel + float(quarter) >= edge,
-                  pixel < edge, pixel + float(quarter) < edge)
-        parts = [jnp.maximum(jnp.where(ok, p, 0.0), 0.0) for ok, p in zip(inside, (p0, p1, p2, p3))]
-        return jnp.concatenate([p * p for p in parts], axis=0)
-
-    def with_rest(value):
-        return value, value - value.astype(jnp.bfloat16).astype(jnp.float32)
+        here = pixel >= edge
+        s = jnp.where(here, unit, unit + 1.0) - centre
+        p = jnp.maximum(h2 - s * s, 0.0)
+        return here, p * p
+
+    def laid_out(here, value):
+        return jnp.concatenate([jnp.where(here, value, 0.0), jnp.where(here, 0.0, value)], axis=0)
+
+    def with_rest(here, value):
+        rest = value - value.astype(jnp.bfloat16).astype(jnp.float32)
+        return laid_out(here, value), laid_out(here, rest)
 
     def factors(row):
         def param(k):
             return prep[k, pl.ds(row, 1), :]
 
         h2 = param(4)
-        across = bump(param(0), param(1), h2)
-        down = bump(param(2), param(3), h2)
-        spread = jnp.concatenate([across * param(5 + c) for c in range(4)], axis=0)
-        lhs = jnp.concatenate(with_rest(spread), axis=1)
+        here_x, across = bump(param(0), param(1), h2)
+        here_y, down = bump(param(2), param(3), h2)
+        lhs = jnp.concatenate(
+            [jnp.concatenate(with_rest(here_x, across * param(5 + c)), axis=1) for c in range(4)],
+            axis=0)
         rhs = jnp.concatenate(
-            [jnp.concatenate([part, part], axis=1) for part in with_rest(down)], axis=0)
+            [jnp.concatenate([part, part], axis=1) for part in with_rest(here_y, down)], axis=0)
         return lhs, rhs
 
     def product(lhs, rhs):

time: 94.1 us -> 93.8 us (level); the launches traced: 96 us -> 92.9 us
  starting transfers between devices: 23.1 us -> 15.6 us
  waiting for transfers between devices: 43.9 us -> 46.9 us
  Pallas kernels: 25 us -> 26.4 us
    ppermute x3, starting transfers between devices: 6.14 us -> 2.08 us  [shards(): lax.ppermute(partial[k], 'screen', [(i, (i + k) % screen_size) for i in r...]
    ppermute x3, waiting for transfers between devices: 38.7 us -> 42.2 us  [shards(): lax.ppermute(partial[k], 'screen', [(i, (i + k) % screen_size) for i in r...]
    ppermute x7, starting transfers between devices: 17 us -> 13.5 us  [shards(): lax.ppermute(block, 'depth', [(i, i ^ k) for i in range(depth_size)])]
    pallas_call x1, Pallas kernels: 25 us -> 26.4 us  [deposit(): pl.pallas_call(functools.partial(deposit_kernel, tiles_all, slots, pb, sc...]
  transfers between devices with their start and end apart: 10 -> 10, of which waited for: 4 -> 5; matrix products, arithmetic and copies ran while one was open for 1% -> 1% of each run, Pallas kernels for 0% -> 0%
where the time goes in v4:
time: 93.8 us; the launch traced here: 92.9 us
  waiting for transfers between devices  46.9 us (50%)
  Pallas kernels  26.4 us (28%)
  starting transfers between devices  15.6 us (17%)
  other arithmetic  2.2 us (2%)
  local copies, waits for them, and re-layouts  0.96 us (1%)
    ppermute x3, waiting for transfers between devices, shards(): lax.ppermute(partial[k], 'screen', [(i, (i + k) % screen_size) for i in r...  42.2 us
    pallas_call x1, Pallas kernels, deposit(): pl.pallas_call(functools.partial(deposit_kernel, tiles_all, slots, pb, sc...  26.4 us
    ppermute x7, starting transfers between devices, shards(): lax.ppermute(block, 'depth', [(i, i ^ k) for i in range(depth_size)])  13.5 us
    ppermute x7, waiting for transfers between devices, shards(): lax.ppermute(block, 'depth', [(i, i ^ k) for i in range(depth_size)])  4.71 us
    ppermute x3, starting transfers between devices, shards(): lax.ppermute(partial[k], 'screen', [(i, (i + k) % screen_size) for i in r...  2.08 us
  transfers between devices with their start and end apart: 10, of which 5 were waited for; matrix products, arithmetic and copies ran while one was open for 1% of the time, Pallas kernels for 0%

profile of v4, /device:TPU:0, one launch (start us, length us, event | category | flops | bytes accessed | tf_op | source)
XLA Modules:
  0.0 92.9 jit_solution(14422003479889402260)
XLA Ops:
  0.7 26.4 %deposit.1 = (f32[8,128,128]{2,1,0:T(8,128)}, f32[8,128,128]{2,1,0:T(8,128)}, f32[8,128,128]{2,1,0:T(8,128)}, f32[8,128,128]{2,1,0:T(8,128)}) custom-call(s32[1,1]{1,0:T(1,128)S(6)} %copy.21.count_ref, s32[1,1]{1,0:T(1,128)} %bitcast.2.place_ref, s32[1,2048]{1,0:T(1,128)} %tile_hbm.1, s32[2,1,2048,128]{3,2,1,0:T(8,128)} %corner_hbm.1, ...), custom_call_target="tpu_custom_call" | custom-call | tf_op jit(solution)/shard_map/deposit/pallas_call | solution.py:176
  27.1 1.1 %collective-permute-start.2 = (f32[8,128,128]{2,1,0:T(8,128)}, f32[8,128,128]{2,1,0:T(8,128)S(1)}, u32[]{:S(2)}, u32[]{:S(2)}) collective-permute-start(f32[8,128,128]{2,1,0:T(8,128)} %get-tuple-element.12), channel_id=1, source_target_pairs={{0,3},{1,0},{2,1},{3,2},{4,7},{5,4},{6,5},{7,6},{8,11},{9,8},{10,9... | collective-permute-start | bytes 1572872 | tf_op jit(solution)/shard_map/ppermute | solution.py:227
  28.2 0.9 %collective-permute-start = (f32[8,128,128]{2,1,0:T(8,128)}, f32[8,128,128]{2,1,0:T(8,128)S(1)}, u32[]{:S(2)}, u32[]{:S(2)}) collective-permute-start(f32[8,128,128]{2,1,0:T(8,128)} %get-tuple-element.10), channel_id=1, source_target_pairs={{0,1},{1,2},{2,3},{3,0},{4,5},{5,6},{6,7},{7,4},{8,9},{9,10},{10,1... | collective-permute-start | bytes 1572872 | tf_op jit(solution)/shard_map/ppermute | solution.py:227
  29.2 0.6 gather_fusion
  29.8 0.1 compare_convert_fusion
  29.9 11.0 %collective-permute-done.2 = f32[8,128,128]{2,1,0:T(8,128)S(1)} collective-permute-done((f32[8,128,128]{2,1,0:T(8,128)}, f32[8,128,128]{2,1,0:T(8,128)S(1)}, u32[]{:S(2)}, u32[]{:S(2)}) %collective-permute-start.2) | collective-permute-done | bytes 524320 | tf_op jit(solution)/shard_map/ppermute | solution.py:227
  40.9 31.2 %collective-permute-done.1 = f32[8,128,128]{2,1,0:T(8,128)S(1)} collective-permute-done((f32[8,128,128]{2,1,0:T(8,128)}, f32[8,128,128]{2,1,0:T(8,128)S(1)}, u32[]{:S(2)}, u32[]{:S(2)}) %collective-permute-start.1) | collective-permute-done | bytes 524320 | tf_op jit(solution)/shard_map/ppermute | solution.py:227
  72.1 0.0 collective-permute-done
  72.1 1.2 %add_add_fusion = f32[8,128,128]{2,1,0:T(8,128)S(1)} fusion(f32[8,128,128]{2,1,0:T(8,128)S(1)} %collective-permute-done.2, f32[8,128,128]{2,1,0:T(8,128)S(1)} %collective-permute-done.1, f32[8,128,128]{2,1,0:T(8,128)} %get-tuple-element.9, f32[8,128,128]{2,1,0:T(8,128)S(1)} %collective-permute-done), kind=kLoop, calls=%fused_computation.1 | loop fusion | flops 393216 | bytes 2621440 | tf_op jit(solution)/shard_map/add | solution.py:231
  73.3 0.1 constant_dynamic-slice_fusion
  73.4 0.4 collective-permute-start.3
  73.8 8.6 %collective-permute-start.4 = (f32[1,128,128]{2,1,0:T(8,128)S(1)}, f32[1,128,128]{2,1,0:T(8,128)S(1)}, u32[]{:S(2)}, u32[]{:S(2)}) collective-permute-start(f32[1,128,128]{2,1,0:T(8,128)S(1)} %get-tuple-element.20), channel_id=1, source_target_pairs={{0,8},{4,12},{8,0},{12,4},{16,24},{20,28},{24,16},{28,20},{1,9},{5... | collective-permute-start | bytes 196616 | tf_op jit(solution)/shard_map/ppermute | solution.py:236
  82.4 0.0 collective-permute-start.5
  82.4 1.4 %collective-permute-start.6 = (f32[1,128,128]{2,1,0:T(8,128)S(1)}, f32[1,128,128]{2,1,0:T(8,128)S(1)}, u32[]{:S(2)}, u32[]{:S(2)}) collective-permute-start(f32[1,128,128]{2,1,0:T(8,128)S(1)} %get-tuple-element.18), channel_id=1, source_target_pairs={{0,16},{4,20},{8,24},{12,28},{16,0},{20,4},{24,8},{28,12},{1,17},{... | collective-permute-start | bytes 196616 | tf_op jit(solution)/shard_map/ppermute | solution.py:236
  83.8 0.1 collective-permute-start.7
  83.9 2.7 %collective-permute-start.8 = (f32[1,128,128]{2,1,0:T(8,128)S(1)}, f32[1,128,128]{2,1,0:T(8,128)S(1)}, u32[]{:S(2)}, u32[]{:S(2)}) collective-permute-start(f32[1,128,128]{2,1,0:T(8,128)S(1)} %get-tuple-element.16), channel_id=1, source_target_pairs={{0,24},{4,28},{8,16},{12,20},{16,8},{20,12},{24,0},{28,4},{1,25},{... | collective-permute-start | bytes 196616 | tf_op jit(solution)/shard_map/ppermute | solution.py:236
  86.7 0.2 collective-permute-start.9
  87.0 1.1 %collective-permute-done.7 = f32[1,128,128]{2,1,0:T(8,128)S(1)} collective-permute-done((f32[1,128,128]{2,1,0:T(8,128)S(1)}, f32[1,128,128]{2,1,0:T(8,128)S(1)}, u32[]{:S(2)}, u32[]{:S(2)}) %collective-permute-start.7) | collective-permute-done | bytes 65568 | tf_op jit(solution)/shard_map/ppermute | solution.py:236
  88.1 1.4 %collective-permute-done.8 = f32[1,128,128]{2,1,0:T(8,128)S(1)} collective-permute-done((f32[1,128,128]{2,1,0:T(8,128)S(1)}, f32[1,128,128]{2,1,0:T(8,128)S(1)}, u32[]{:S(2)}, u32[]{:S(2)}) %collective-permute-start.8) | collective-permute-done | bytes 65568 | tf_op jit(solution)/shard_map/ppermute | solution.py:236
  89.6 2.1 %collective-permute-done.9 = f32[1,128,128]{2,1,0:T(8,128)S(1)} collective-permute-done((f32[1,128,128]{2,1,0:T(8,128)S(1)}, f32[1,128,128]{2,1,0:T(8,128)S(1)}, u32[]{:S(2)}, u32[]{:S(2)}) %collective-permute-start.9) | collective-permute-done | bytes 65568 | tf_op jit(solution)/shard_map/ppermute | solution.py:236
  91.7 0.2 exponential_multiply_fusion
  91.9 0.1 copy.13
  92.0 0.1 copy.11
  92.1 0.7 maximum_bitcast_fusion
  (27 shorter events, 0.1 us)
Async XLA Ops:
  0.0 29.2 %copy-start = (s32[8]{0:T(128)S(1)}, s32[8]{0:T(128)}, u32[]{:S(2)}) copy-start(s32[8]{0:T(128)} %param.10) | copy-start | bytes 100
  27.1 13.8 %collective-permute-start.2 = (f32[8,128,128]{2,1,0:T(8,128)}, f32[8,128,128]{2,1,0:T(8,128)S(1)}, u32[]{:S(2)}, u32[]{:S(2)}) collective-permute-start(f32[8,128,128]{2,1,0:T(8,128)} %get-tuple-element.12), channel_id=1, source_target_pairs={{0,3},{1,0},{2,1},{3,2},{4,7},{5,4},{6,5},{7,6},{8,11},{9,8},{10,9... | collective-permute-start | bytes 1572872 | tf_op jit(solution)/shard_map/ppermute | solution.py:227
  28.2 43.9 %collective-permute-start.1 = (f32[8,128,128]{2,1,0:T(8,128)}, f32[8,128,128]{2,1,0:T(8,128)S(1)}, u32[]{:S(2)}, u32[]{:S(2)}) collective-permute-start(f32[8,128,128]{2,1,0:T(8,128)} %get-tuple-element.11), channel_id=1, source_target_pairs={{0,2},{1,3},{2,0},{3,1},{4,6},{5,7},{6,4},{7,5},{8,10},{9,11},{10,... | collective-permute-start | bytes 1572872 | tf_op jit(solution)/shard_map/ppermute | solution.py:227
  28.2 43.9 %collective-permute-start = (f32[8,128,128]{2,1,0:T(8,128)}, f32[8,128,128]{2,1,0:T(8,128)S(1)}, u32[]{:S(2)}, u32[]{:S(2)}) collective-permute-start(f32[8,128,128]{2,1,0:T(8,128)} %get-tuple-element.10), channel_id=1, source_target_pairs={{0,1},{1,2},{2,3},{3,0},{4,5},{5,6},{6,7},{7,4},{8,9},{9,10},{10,1... | collective-permute-start | bytes 1572872 | tf_op jit(solution)/shard_map/ppermute | solution.py:227
  73.4 10.6 %collective-permute-start.3 = (f32[1,128,128]{2,1,0:T(8,128)S(1)}, f32[1,128,128]{2,1,0:T(8,128)S(1)}, u32[]{:S(2)}, u32[]{:S(2)}) collective-permute-start(f32[1,128,128]{2,1,0:T(8,128)S(1)} %get-tuple-element.21), channel_id=1, source_target_pairs={{0,4},{4,0},{8,12},{12,8},{16,20},{20,16},{24,28},{28,24},{1,5},{5... | collective-permute-start | bytes 196616 | tf_op jit(solution)/shard_map/ppermute | solution.py:236
  73.8 12.9 %collective-permute-start.4 = (f32[1,128,128]{2,1,0:T(8,128)S(1)}, f32[1,128,128]{2,1,0:T(8,128)S(1)}, u32[]{:S(2)}, u32[]{:S(2)}) collective-permute-start(f32[1,128,128]{2,1,0:T(8,128)S(1)} %get-tuple-element.20), channel_id=1, source_target_pairs={{0,8},{4,12},{8,0},{12,4},{16,24},{20,28},{24,16},{28,20},{1,9},{5... | collective-permute-start | bytes 196616 | tf_op jit(solution)/shard_map/ppermute | solution.py:236
  82.4 4.5 %collective-permute-start.5 = (f32[1,128,128]{2,1,0:T(8,128)S(1)}, f32[1,128,128]{2,1,0:T(8,128)S(1)}, u32[]{:S(2)}, u32[]{:S(2)}) collective-permute-start(f32[1,128,128]{2,1,0:T(8,128)S(1)} %get-tuple-element.19), channel_id=1, source_target_pairs={{0,12},{4,8},{8,4},{12,0},{16,28},{20,24},{24,20},{28,16},{1,13},{... | collective-permute-start | bytes 196616 | tf_op jit(solution)/shard_map/ppermute | solution.py:236
  82.4 4.5 %collective-permute-start.6 = (f32[1,128,128]{2,1,0:T(8,128)S(1)}, f32[1,128,128]{2,1,0:T(8,128)S(1)}, u32[]{:S(2)}, u32[]{:S(2)}) collective-permute-start(f32[1,128,128]{2,1,0:T(8,128)S(1)} %get-tuple-element.18), channel_id=1, source_target_pairs={{0,16},{4,20},{8,24},{12,28},{16,0},{20,4},{24,8},{28,12},{1,17},{... | collective-permute-start | bytes 196616 | tf_op jit(solution)/shard_map/ppermute | solution.py:236
  83.8 4.3 %collective-permute-start.7 = (f32[1,128,128]{2,1,0:T(8,128)S(1)}, f32[1,128,128]{2,1,0:T(8,128)S(1)}, u32[]{:S(2)}, u32[]{:S(2)}) collective-permute-start(f32[1,128,128]{2,1,0:T(8,128)S(1)} %get-tuple-element.17), channel_id=1, source_target_pairs={{0,20},{4,16},{8,28},{12,24},{16,4},{20,0},{24,12},{28,8},{1,21},{... | collective-permute-start | bytes 196616 | tf_op jit(solution)/shard_map/ppermute | solution.py:236
  83.9 5.6 %collective-permute-start.8 = (f32[1,128,128]{2,1,0:T(8,128)S(1)}, f32[1,128,128]{2,1,0:T(8,128)S(1)}, u32[]{:S(2)}, u32[]{:S(2)}) collective-permute-start(f32[1,128,128]{2,1,0:T(8,128)S(1)} %get-tuple-element.16), channel_id=1, source_target_pairs={{0,24},{4,28},{8,16},{12,20},{16,8},{20,12},{24,0},{28,4},{1,25},{... | collective-permute-start | bytes 196616 | tf_op jit(solution)/shard_map/ppermute | solution.py:236
  86.7 5.0 %collective-permute-start.9 = (f32[1,128,128]{2,1,0:T(8,128)S(1)}, f32[1,128,128]{2,1,0:T(8,128)S(1)}, u32[]{:S(2)}, u32[]{:S(2)}) collective-permute-start(f32[1,128,128]{2,1,0:T(8,128)S(1)} %get-tuple-element.15), channel_id=1, source_target_pairs={{0,28},{4,24},{8,20},{12,16},{16,12},{20,8},{24,4},{28,0},{1,29},{... | collective-permute-start | bytes 196616 | tf_op jit(solution)/shard_map/ppermute | solution.py:236

commit v5 on v4

--- a/solution.py
+++ b/solution.py
@@ -10,8 +10,8 @@
 TS = 32
 FOOT = 16
 TILE_DEV = 4
-N_CHUNK = 16
-UNROLL = 128
+N_CHUNK = 8
+UNROLL = 256
 SKEW = 4
 
 

time: 93.8 us -> 90.4 us (0.964); the launches traced: 92.9 us -> 91 us
  Pallas kernels: 26.4 us -> 19.1 us
  starting transfers between devices: 15.6 us -> 21 us
    ppermute x3, starting transfers between devices: 2.08 us -> 14.6 us  [shards(): lax.ppermute(partial[k], 'screen', [(i, (i + k) % screen_size) for i in r...]
    pallas_call x1, Pallas kernels: 26.4 us -> 19.1 us  [deposit(): pl.pallas_call(functools.partial(deposit_kernel, tiles_all, slots, pb, sc...]
    ppermute x7, starting transfers between devices: 13.5 us -> 6.37 us  [shards(): lax.ppermute(block, 'depth', [(i, i ^ k) for i in range(depth_size)])]
    ppermute x3, waiting for transfers between devices: 42.2 us -> 43.2 us  [shards(): lax.ppermute(partial[k], 'screen', [(i, (i + k) % screen_size) for i in r...]
    ppermute x7, waiting for transfers between devices: 4.71 us -> 3.73 us  [shards(): lax.ppermute(block, 'depth', [(i, i ^ k) for i in range(depth_size)])]
  transfers between devices with their start and end apart: 10 -> 10, of which waited for: 5 -> 6; matrix products, arithmetic and copies ran while one was open for 1% -> 1% of each run, Pallas kernels for 0% -> 0%
where the time goes in v5:
time: 90.4 us; the launch traced here: 91 us
  waiting for transfers between devices  47 us (52%)
  starting transfers between devices  21 us (23%)
  Pallas kernels  19.1 us (21%)
  other arithmetic  2.2 us (2%)
  local copies, waits for them, and re-layouts  0.95 us (1%)
    ppermute x3, waiting for transfers between devices, shards(): lax.ppermute(partial[k], 'screen', [(i, (i + k) % screen_size) for i in r...  43.2 us
    pallas_call x1, Pallas kernels, deposit(): pl.pallas_call(functools.partial(deposit_kernel, tiles_all, slots, pb, sc...  19.1 us
    ppermute x3, starting transfers between devices, shards(): lax.ppermute(partial[k], 'screen', [(i, (i + k) % screen_size) for i in r...  14.6 us
    ppermute x7, starting transfers between devices, shards(): lax.ppermute(block, 'depth', [(i, i ^ k) for i in range(depth_size)])  6.37 us
    ppermute x7, waiting for transfers between devices, shards(): lax.ppermute(block, 'depth', [(i, i ^ k) for i in range(depth_size)])  3.73 us
  transfers between devices with their start and end apart: 10, of which 6 were waited for; matrix products, arithmetic and copies ran while one was open for 1% of the time, Pallas kernels for 0%

profile of v5, /device:TPU:0, one launch (start us, length us, event | category | flops | bytes accessed | tf_op | source)
XLA Modules:
  0.0 91.0 jit_solution(15747171332597784001)
XLA Ops:
  0.7 19.1 %deposit.1 = (f32[8,128,128]{2,1,0:T(8,128)}, f32[8,128,128]{2,1,0:T(8,128)}, f32[8,128,128]{2,1,0:T(8,128)}, f32[8,128,128]{2,1,0:T(8,128)}) custom-call(s32[1,1]{1,0:T(1,128)S(6)} %copy.21.count_ref, s32[1,1]{1,0:T(1,128)} %bitcast.2.place_ref, s32[1,2048]{1,0:T(1,128)} %tile_hbm.1, s32[2,1,2048,128]{3,2,1,0:T(8,128)} %corner_hbm.1, ...), custom_call_target="tpu_custom_call" | custom-call | tf_op jit(solution)/shard_map/deposit/pallas_call | solution.py:176
  19.8 5.1 %collective-permute-start.2 = (f32[8,128,128]{2,1,0:T(8,128)}, f32[8,128,128]{2,1,0:T(8,128)S(1)}, u32[]{:S(2)}, u32[]{:S(2)}) collective-permute-start(f32[8,128,128]{2,1,0:T(8,128)} %get-tuple-element.12), channel_id=1, source_target_pairs={{0,3},{1,0},{2,1},{3,2},{4,7},{5,4},{6,5},{7,6},{8,11},{9,8},{10,9... | collective-permute-start | bytes 1572872 | tf_op jit(solution)/shard_map/ppermute | solution.py:227
  24.9 7.6 %collective-permute-start.1 = (f32[8,128,128]{2,1,0:T(8,128)}, f32[8,128,128]{2,1,0:T(8,128)S(1)}, u32[]{:S(2)}, u32[]{:S(2)}) collective-permute-start(f32[8,128,128]{2,1,0:T(8,128)} %get-tuple-element.11), channel_id=1, source_target_pairs={{0,2},{1,3},{2,0},{3,1},{4,6},{5,7},{6,4},{7,5},{8,10},{9,11},{10,... | collective-permute-start | bytes 1572872 | tf_op jit(solution)/shard_map/ppermute | solution.py:227
  32.5 1.9 %collective-permute-start = (f32[8,128,128]{2,1,0:T(8,128)}, f32[8,128,128]{2,1,0:T(8,128)S(1)}, u32[]{:S(2)}, u32[]{:S(2)}) collective-permute-start(f32[8,128,128]{2,1,0:T(8,128)} %get-tuple-element.10), channel_id=1, source_target_pairs={{0,1},{1,2},{2,3},{3,0},{4,5},{5,6},{6,7},{7,4},{8,9},{9,10},{10,1... | collective-permute-start | bytes 1572872 | tf_op jit(solution)/shard_map/ppermute | solution.py:227
  34.4 0.6 gather_fusion
  35.1 0.1 compare_convert_fusion
  35.2 2.2 %collective-permute-done.2 = f32[8,128,128]{2,1,0:T(8,128)S(1)} collective-permute-done((f32[8,128,128]{2,1,0:T(8,128)}, f32[8,128,128]{2,1,0:T(8,128)S(1)}, u32[]{:S(2)}, u32[]{:S(2)}) %collective-permute-start.2) | collective-permute-done | bytes 524320 | tf_op jit(solution)/shard_map/ppermute | solution.py:227
  37.3 41.1 %collective-permute-done.1 = f32[8,128,128]{2,1,0:T(8,128)S(1)} collective-permute-done((f32[8,128,128]{2,1,0:T(8,128)}, f32[8,128,128]{2,1,0:T(8,128)S(1)}, u32[]{:S(2)}, u32[]{:S(2)}) %collective-permute-start.1) | collective-permute-done | bytes 524320 | tf_op jit(solution)/shard_map/ppermute | solution.py:227
  78.4 1.2 %add_add_fusion = f32[8,128,128]{2,1,0:T(8,128)S(1)} fusion(f32[8,128,128]{2,1,0:T(8,128)S(1)} %collective-permute-done.2, f32[8,128,128]{2,1,0:T(8,128)S(1)} %collective-permute-done.1, f32[8,128,128]{2,1,0:T(8,128)} %get-tuple-element.9, f32[8,128,128]{2,1,0:T(8,128)S(1)} %collective-permute-done), kind=kLoop, calls=%fused_computation.1 | loop fusion | flops 393216 | bytes 2621440 | tf_op jit(solution)/shard_map/add | solution.py:231
  79.6 0.1 constant_dynamic-slice_fusion
  79.7 0.1 collective-permute-start.3
  79.7 1.4 %collective-permute-start.4 = (f32[1,128,128]{2,1,0:T(8,128)S(1)}, f32[1,128,128]{2,1,0:T(8,128)S(1)}, u32[]{:S(2)}, u32[]{:S(2)}) collective-permute-start(f32[1,128,128]{2,1,0:T(8,128)S(1)} %get-tuple-element.20), channel_id=1, source_target_pairs={{0,8},{4,12},{8,0},{12,4},{16,24},{20,28},{24,16},{28,20},{1,9},{5... | collective-permute-start | bytes 196616 | tf_op jit(solution)/shard_map/ppermute | solution.py:236
  81.1 0.5 collective-permute-start.5
  81.6 1.7 %collective-permute-start.7 = (f32[1,128,128]{2,1,0:T(8,128)S(1)}, f32[1,128,128]{2,1,0:T(8,128)S(1)}, u32[]{:S(2)}, u32[]{:S(2)}) collective-permute-start(f32[1,128,128]{2,1,0:T(8,128)S(1)} %get-tuple-element.17), channel_id=1, source_target_pairs={{0,20},{4,16},{8,28},{12,24},{16,4},{20,0},{24,12},{28,8},{1,21},{... | collective-permute-start | bytes 196616 | tf_op jit(solution)/shard_map/ppermute | solution.py:236
  83.3 1.1 %collective-permute-start.8 = (f32[1,128,128]{2,1,0:T(8,128)S(1)}, f32[1,128,128]{2,1,0:T(8,128)S(1)}, u32[]{:S(2)}, u32[]{:S(2)}) collective-permute-start(f32[1,128,128]{2,1,0:T(8,128)S(1)} %get-tuple-element.16), channel_id=1, source_target_pairs={{0,24},{4,28},{8,16},{12,20},{16,8},{20,12},{24,0},{28,4},{1,25},{... | collective-permute-start | bytes 196616 | tf_op jit(solution)/shard_map/ppermute | solution.py:236
  84.5 1.6 %collective-permute-start.9 = (f32[1,128,128]{2,1,0:T(8,128)S(1)}, f32[1,128,128]{2,1,0:T(8,128)S(1)}, u32[]{:S(2)}, u32[]{:S(2)}) collective-permute-start(f32[1,128,128]{2,1,0:T(8,128)S(1)} %get-tuple-element.15), channel_id=1, source_target_pairs={{0,28},{4,24},{8,20},{12,16},{16,12},{20,8},{24,4},{28,0},{1,29},{... | collective-permute-start | bytes 196616 | tf_op jit(solution)/shard_map/ppermute | solution.py:236
  86.1 0.4 collective-permute-done.6
  86.6 0.4 collective-permute-done.7
  87.0 2.0 %collective-permute-done.8 = f32[1,128,128]{2,1,0:T(8,128)S(1)} collective-permute-done((f32[1,128,128]{2,1,0:T(8,128)S(1)}, f32[1,128,128]{2,1,0:T(8,128)S(1)}, u32[]{:S(2)}, u32[]{:S(2)}) %collective-permute-start.8) | collective-permute-done | bytes 65568 | tf_op jit(solution)/shard_map/ppermute | solution.py:236
  89.0 0.9 collective-permute-done.9
  89.9 0.2 exponential_multiply_fusion
  90.1 0.1 copy.13
  90.2 0.1 copy.11
  90.3 0.7 maximum_bitcast_fusion
  (27 shorter events, 0.1 us)
Async XLA Ops:
  0.0 34.4 %copy-start = (s32[8]{0:T(128)S(1)}, s32[8]{0:T(128)}, u32[]{:S(2)}) copy-start(s32[8]{0:T(128)} %param.10) | copy-start | bytes 100
  19.8 17.6 %collective-permute-start.2 = (f32[8,128,128]{2,1,0:T(8,128)}, f32[8,128,128]{2,1,0:T(8,128)S(1)}, u32[]{:S(2)}, u32[]{:S(2)}) collective-permute-start(f32[8,128,128]{2,1,0:T(8,128)} %get-tuple-element.12), channel_id=1, source_target_pairs={{0,3},{1,0},{2,1},{3,2},{4,7},{5,4},{6,5},{7,6},{8,11},{9,8},{10,9... | collective-permute-start | bytes 1572872 | tf_op jit(solution)/shard_map/ppermute | solution.py:227
  24.9 53.5 %collective-permute-start.1 = (f32[8,128,128]{2,1,0:T(8,128)}, f32[8,128,128]{2,1,0:T(8,128)S(1)}, u32[]{:S(2)}, u32[]{:S(2)}) collective-permute-start(f32[8,128,128]{2,1,0:T(8,128)} %get-tuple-element.11), channel_id=1, source_target_pairs={{0,2},{1,3},{2,0},{3,1},{4,6},{5,7},{6,4},{7,5},{8,10},{9,11},{10,... | collective-permute-start | bytes 1572872 | tf_op jit(solution)/shard_map/ppermute | solution.py:227
  32.5 45.9 %collective-permute-start = (f32[8,128,128]{2,1,0:T(8,128)}, f32[8,128,128]{2,1,0:T(8,128)S(1)}, u32[]{:S(2)}, u32[]{:S(2)}) collective-permute-start(f32[8,128,128]{2,1,0:T(8,128)} %get-tuple-element.10), channel_id=1, source_target_pairs={{0,1},{1,2},{2,3},{3,0},{4,5},{5,6},{6,7},{7,4},{8,9},{9,10},{10,1... | collective-permute-start | bytes 1572872 | tf_op jit(solution)/shard_map/ppermute | solution.py:227
  79.7 3.6 %collective-permute-start.3 = (f32[1,128,128]{2,1,0:T(8,128)S(1)}, f32[1,128,128]{2,1,0:T(8,128)S(1)}, u32[]{:S(2)}, u32[]{:S(2)}) collective-permute-start(f32[1,128,128]{2,1,0:T(8,128)S(1)} %get-tuple-element.21), channel_id=1, source_target_pairs={{0,4},{4,0},{8,12},{12,8},{16,20},{20,16},{24,28},{28,24},{1,5},{5... | collective-permute-start | bytes 196616 | tf_op jit(solution)/shard_map/ppermute | solution.py:236
  79.7 4.7 %collective-permute-start.4 = (f32[1,128,128]{2,1,0:T(8,128)S(1)}, f32[1,128,128]{2,1,0:T(8,128)S(1)}, u32[]{:S(2)}, u32[]{:S(2)}) collective-permute-start(f32[1,128,128]{2,1,0:T(8,128)S(1)} %get-tuple-element.20), channel_id=1, source_target_pairs={{0,8},{4,12},{8,0},{12,4},{16,24},{20,28},{24,16},{28,20},{1,9},{5... | collective-permute-start | bytes 196616 | tf_op jit(solution)/shard_map/ppermute | solution.py:236
  81.1 5.0 %collective-permute-start.5 = (f32[1,128,128]{2,1,0:T(8,128)S(1)}, f32[1,128,128]{2,1,0:T(8,128)S(1)}, u32[]{:S(2)}, u32[]{:S(2)}) collective-permute-start(f32[1,128,128]{2,1,0:T(8,128)S(1)} %get-tuple-element.19), channel_id=1, source_target_pairs={{0,12},{4,8},{8,4},{12,0},{16,28},{20,24},{24,20},{28,16},{1,13},{... | collective-permute-start | bytes 196616 | tf_op jit(solution)/shard_map/ppermute | solution.py:236
  81.6 5.0 %collective-permute-start.6 = (f32[1,128,128]{2,1,0:T(8,128)S(1)}, f32[1,128,128]{2,1,0:T(8,128)S(1)}, u32[]{:S(2)}, u32[]{:S(2)}) collective-permute-start(f32[1,128,128]{2,1,0:T(8,128)S(1)} %get-tuple-element.18), channel_id=1, source_target_pairs={{0,16},{4,20},{8,24},{12,28},{16,0},{20,4},{24,8},{28,12},{1,17},{... | collective-permute-start | bytes 196616 | tf_op jit(solution)/shard_map/ppermute | solution.py:236
  81.6 5.4 %collective-permute-start.7 = (f32[1,128,128]{2,1,0:T(8,128)S(1)}, f32[1,128,128]{2,1,0:T(8,128)S(1)}, u32[]{:S(2)}, u32[]{:S(2)}) collective-permute-start(f32[1,128,128]{2,1,0:T(8,128)S(1)} %get-tuple-element.17), channel_id=1, source_target_pairs={{0,20},{4,16},{8,28},{12,24},{16,4},{20,0},{24,12},{28,8},{1,21},{... | collective-permute-start | bytes 196616 | tf_op jit(solution)/shard_map/ppermute | solution.py:236
  83.3 5.7 %collective-permute-start.8 = (f32[1,128,128]{2,1,0:T(8,128)S(1)}, f32[1,128,128]{2,1,0:T(8,128)S(1)}, u32[]{:S(2)}, u32[]{:S(2)}) collective-permute-start(f32[1,128,128]{2,1,0:T(8,128)S(1)} %get-tuple-element.16), channel_id=1, source_target_pairs={{0,24},{4,28},{8,16},{12,20},{16,8},{20,12},{24,0},{28,4},{1,25},{... | collective-permute-start | bytes 196616 | tf_op jit(solution)/shard_map/ppermute | solution.py:236
  84.5 5.4 %collective-permute-start.9 = (f32[1,128,128]{2,1,0:T(8,128)S(1)}, f32[1,128,128]{2,1,0:T(8,128)S(1)}, u32[]{:S(2)}, u32[]{:S(2)}) collective-permute-start(f32[1,128,128]{2,1,0:T(8,128)S(1)} %get-tuple-element.15), channel_id=1, source_target_pairs={{0,28},{4,24},{8,20},{12,16},{16,12},{20,8},{24,4},{28,0},{1,29},{... | collective-permute-start | bytes 196616 | tf_op jit(solution)/shard_map/ppermute | solution.py:236
